TPU v7x, 256 devices: a whole 4x4x8 slice. The times are simulated.
256 devices in a mesh: dp: 16 (over z, core), seq: 16 (over y, x).
Axes of the slice: x: 4, y: 4, z: 8, core: 2. Of those that a mesh axis runs over, the one named last changes fastest.
Arguments:
- queries: bfloat16 [32768, 64, 128], P(('dp', 'seq')), parts along dimension 0, may hold values from -52 to 52
- keys: bfloat16 [32768, 8, 128], P(('dp', 'seq')), parts along dimension 0, may hold values from -6 to 6
- values: bfloat16 [32768, 8, 128], P(('dp', 'seq')), parts along dimension 0, may hold values from -6 to 6
- doc_ids: int32 [32768], P(('dp', 'seq')), parts along dimension 0, may hold values from 0 to 15, never falling along the last dimension, each value on 1 to 512 neighbouring positions
- counts: int32 [256], P('dp'), parts along dimension 0, may hold values from 64 to 128
Outputs:
- attended: bfloat16 [32768, 64, 128], P(('dp', 'seq')), parts along dimension 0
There are 16 independent parts, one for each index of `dp`. A program takes and returns all parts, laid end to end along the dimension named above; each array names one. Nothing has to cross between parts.
Inputs may be any that keep to these rules, and one draw needn't show every extreme that they name: `doc_ids`: document numbers never fall along the sequence; each document has 1 to 512 positions. The first counts[j] positions of shard j are real tokens, the others padding.
All inputs are finite; a program needn't handle non-finite values.
Results may differ from a plain program's by a relative error of at most 0.003.
Values may be sent and summed in bfloat16 or wider, within the bound.
No kernel may reach another device: no remote copies, remote signals or barrier semaphores. Data moves between devices by JAX's collectives and lax.ppermute only.
A program may use at most 64 MiB of HBM per device.

v0:
```python
import math

import jax
import jax.numpy as jnp
from jax import lax
from jax.sharding import PartitionSpec as P

DOC_MOST = 512


def from_behind(array, axis, by):
    size = lax.axis_size(axis)
    pairs = [(i, i + by) for i in range(size) if 0 <= i + by < size]
    return lax.ppermute(array, axis, pairs)


def joined_along(parts, dim):
    parts = jnp.moveaxis(parts, 0, dim)
    shape = parts.shape
    return parts.reshape(*shape[:dim], shape[dim] * shape[dim + 1], *shape[dim + 2 :])


def sent_to_all(array, axis):
    size = lax.axis_size(axis)
    return lax.all_to_all(
        jnp.broadcast_to(array[None], (size, *array.shape)), axis, 0, 0, tiled=True
    )


def gather_directly(array, axis, dim):
    return joined_along(sent_to_all(array, axis), dim)


def window_attend(queries, keys, values, all_docs, live_rows, device, shard_rows):
    reach = (DOC_MOST + shard_rows - 1) // shard_rows
    head_size = queries.shape[2]
    kv_heads_all = keys.shape[1]
    queries_per_group = queries.shape[1] // kv_heads_all
    score_scale = 1.0 / math.sqrt(head_size)
    key_parts = []
    value_parts = []
    for offset in range(reach, 0, -1):
        earlier_keys, earlier_values = from_behind((keys, values), "seq", offset)
        key_parts.append(earlier_keys)
        value_parts.append(earlier_values)
    window_keys = jnp.concatenate(key_parts + [keys], axis=0)
    window_values = jnp.concatenate(value_parts + [values], axis=0)
    window_rows = window_keys.shape[0]
    own_start = device * shard_rows
    window_start = own_start - reach * shard_rows
    padded_docs = jnp.concatenate([jnp.full((reach * shard_rows,), -1, jnp.int32), all_docs])
    padded_live = jnp.concatenate([jnp.zeros((reach * shard_rows,), jnp.bool_), live_rows])
    key_doc = lax.dynamic_slice_in_dim(padded_docs, own_start, window_rows, 0)
    key_live = lax.dynamic_slice_in_dim(padded_live, own_start, window_rows, 0)
    key_pos = window_start + jnp.arange(window_rows, dtype=jnp.int32)
    query_pos = own_start + jnp.arange(shard_rows, dtype=jnp.int32)
    query_doc = lax.dynamic_slice_in_dim(all_docs, own_start, shard_rows, 0)
    query_live = lax.dynamic_slice_in_dim(live_rows, own_start, shard_rows, 0)
    allowed = (
        (key_doc[None, :] == query_doc[:, None])
        & (key_pos[None, :] <= query_pos[:, None])
        & key_live[None, :]
        & (key_pos[None, :] >= 0)
    )
    grouped_queries = jnp.transpose(
        queries.reshape(shard_rows, kv_heads_all, queries_per_group, head_size), (1, 0, 2, 3)
    )
    grouped_keys = jnp.transpose(window_keys, (1, 0, 2))
    grouped_values = jnp.transpose(window_values, (1, 0, 2))

    def one_group(operands):
        query_group, key_group, value_group = operands
        scores = (
            jnp.einsum("qgd,kd->gqk", query_group, key_group, preferred_element_type=jnp.float32)
            * score_scale
        )
        masked = jnp.where(allowed[None], scores, -1e30)
        top = jnp.max(masked, axis=-1, keepdims=True)
        weights = jnp.where(allowed[None], jnp.exp(scores - top), 0.0)
        norm_sum = jnp.sum(weights, axis=-1)
        mixed = jnp.einsum(
            "gqk,kd->qgd",
            weights.astype(jnp.bfloat16),
            value_group,
            preferred_element_type=jnp.float32,
        )
        norm_rows = jnp.transpose(norm_sum, (1, 0))[:, :, None]
        norm_rows = jnp.where(query_live[:, None, None], norm_rows, 1.0)
        return jnp.where(query_live[:, None, None], mixed / norm_rows, 0.0).astype(jnp.bfloat16)

    outputs = lax.map(one_group, (grouped_queries, grouped_keys, grouped_values))
    return jnp.transpose(outputs, (1, 0, 2, 3)).reshape(
        shard_rows, kv_heads_all * queries_per_group, head_size
    )


def local(queries, keys, values, doc_ids, counts):
    shard_count = lax.axis_size("seq")
    shard_rows = queries.shape[0]
    row_count = shard_rows * shard_count
    device = lax.axis_index("seq")
    all_docs = gather_directly(doc_ids, "seq", 0)
    positions = jnp.arange(row_count, dtype=jnp.int32)
    live_rows = positions % shard_rows < jnp.repeat(
        counts, shard_rows, total_repeat_length=row_count
    )
    return window_attend(queries, keys, values, all_docs, live_rows, device, shard_rows)


def solution(mesh):
    in_specs = (
        P(("dp", "seq"), None, None),
        P(("dp", "seq"), None, None),
        P(("dp", "seq"), None, None),
        P(("dp", "seq")),
        P("dp"),
    )
    out_specs = P(("dp", "seq"), None, None)
    return jax.shard_map(local, mesh=mesh, in_specs=in_specs, out_specs=out_specs, check_vma=False)
```

profile of v0, /device:TPU:232, one launch (start us, length us, event | category | flops | bytes accessed | tf_op | source)
XLA Modules:
  0.0 115.9 jit_solution(11350169015695362645)
XLA Ops:
  0.0 1.1 copy.7
  1.2 3.5 %collective-permute-start = (bf16[128,8,128]{0,2,1:T(8,128)(2,1)S(1)}, bf16[128,8,128]{0,2,1:T(8,128)(2,1)}, u32[]{:S(2)}, u32[]{:S(2)}) collective-permute-start(bf16[128,8,128]{0,2,1:T(8,128)(2,1)S(1)} %copy.7), channel_id=1, source_target_pairs={{0,4},{1,5},{2,6},{3,7},{4,8},{5,9},{6,10},{7,11},{8,12},{9,13},{1... | collective-permute-start | bytes 786440 | tf_op jit(solution)/shard_map/ppermute | solution.py:14
  4.6 4.7 %collective-permute-start.1 = (bf16[128,8,128]{0,2,1:T(8,128)(2,1)S(1)}, bf16[128,8,128]{0,2,1:T(8,128)(2,1)}, u32[]{:S(2)}, u32[]{:S(2)}) collective-permute-start(bf16[128,8,128]{0,2,1:T(8,128)(2,1)S(1)} %copy.7), channel_id=1, source_target_pairs={{0,3},{1,4},{2,5},{3,6},{4,7},{5,8},{6,9},{7,10},{8,11},{9,12},{10... | collective-permute-start | bytes 786440 | tf_op jit(solution)/shard_map/ppermute | solution.py:14
  9.3 3.4 %collective-permute-start.2 = (bf16[128,8,128]{0,2,1:T(8,128)(2,1)S(1)}, bf16[128,8,128]{0,2,1:T(8,128)(2,1)S(1)}, u32[]{:S(2)}, u32[]{:S(2)}) collective-permute-start(bf16[128,8,128]{0,2,1:T(8,128)(2,1)S(1)} %copy.7), channel_id=1, source_target_pairs={{0,2},{1,3},{2,4},{3,5},{4,6},{5,7},{6,8},{7,9},{8,10},{9,11},{10,... | collective-permute-start | bytes 786440 | tf_op jit(solution)/shard_map/ppermute | solution.py:14
  12.8 2.8 %collective-permute-start.3 = (bf16[128,8,128]{0,2,1:T(8,128)(2,1)S(1)}, bf16[128,8,128]{0,2,1:T(8,128)(2,1)S(1)}, u32[]{:S(2)}, u32[]{:S(2)}) collective-permute-start(bf16[128,8,128]{0,2,1:T(8,128)(2,1)S(1)} %copy.7), channel_id=1, source_target_pairs={{0,1},{1,2},{2,3},{3,4},{4,5},{5,6},{6,7},{7,8},{8,9},{9,10},{10,1... | collective-permute-start | bytes 786440 | tf_op jit(solution)/shard_map/ppermute | solution.py:14
  15.6 1.3 %broadcast_in_dim.79 = s32[16,1,128]{2,1,0:T(1,128)} broadcast(s32[128]{0:T(128)} %param.12), dimensions={2} | broadcast | bytes 8704 | tf_op jit(solution)/shard_map/broadcast_in_dim | solution.py:26
  16.8 5.1 %all-to-all-start = ((s32[16,1,128]{2,1,0:T(1,128)}), s32[16,1,128]{2,1,0:T(1,128)S(1)}, u32[]{:S(2)}, u32[]{:S(2)}) async-start(s32[16,1,128]{2,1,0:T(1,128)} %broadcast_in_dim.79), calls=%async_computation | async-start | bytes 16384 | tf_op jit(solution)/shard_map/all_to_all | solution.py:25
  21.9 1.0 copy.12
  22.9 3.4 %collective-permute-start.4 = (bf16[128,8,128]{2,0,1:T(8,128)(2,1)S(1)}, bf16[128,8,128]{2,0,1:T(8,128)(2,1)S(1)}, u32[]{:S(2)}, u32[]{:S(2)}) collective-permute-start(bf16[128,8,128]{2,0,1:T(8,128)(2,1)S(1)} %copy.12), channel_id=1, source_target_pairs={{0,4},{1,5},{2,6},{3,7},{4,8},{5,9},{6,10},{7,11},{8,12},{9,13},{1... | collective-permute-start | bytes 786440 | tf_op jit(solution)/shard_map/ppermute | solution.py:14
  26.3 2.0 %fusion.104 = (s32[1]{0:T(128)}, s32[1]{0:T(128)}, s32[1]{0:T(128)}, s32[1]{0:T(128)}, s32[1]{0:T(128)}, /*index=5*/s32[1]{0:T(128)}, s32[1]{0:T(128)}, s32[1]{0...) fusion(s32[16]{0:T(128)} %param.13), kind=kLoop, calls=%fused_computation.85 | loop fusion | bytes 128 | tf_op jit(solution)/shard_map/jit(_take)/gather | solution.py:104
  28.3 4.4 %compare_select_fusion.1 = (s32[2048,1]{0,1:T(1,128)S(1)}, s32[2048,1]{0,1:T(1,128)S(1)}) fusion(s32[]{:T(128)} %bitcast.13, s32[]{:T(128)} %bitcast.14, s32[]{:T(128)} %bitcast.15, s32[]{:T(128)} %bitcast.16, s32[]{:T(128)} %bitcast.17, s32[]{:T(128)} %bitcast.19, s32[]{:T(128)} %bitcast.18, s32[2048,1]{0,1:T(1,128)S(1)} %bitcast.157, ...), kind=kLoop, calls=%fused_computation.52 | loop fusion | flops 28672 | bytes 32796 | tf_op jit(solution)/shard_map/jit(_take)/gather | solution.py:104
  32.9 5.6 %fusion.89 = pred[2048]{0:T(1024)(128)(4,1)S(1)} fusion(pred[2048]{0:T(1024)(128)(4,1)S(1)} %get-tuple-element.95, pred[2048]{0:T(1024)(128)(4,1)S(1)} %get-tuple-element.94, pred[2048]{0:T(1024)(128)(4,1)S(1)} %get-tuple-element.93, pred[2048]{0:T(1024)(128)(4,1)S(1)} %get-tuple-element.92, pred[2048]{0:T(1024)(128)(4,1)S(1)} %get-tuple-element.91, ...), kind=kLoop, calls=%fused_computation.72 | loop fusion | flops 51200 | bytes 28708 | tf_op jit(solution)/shard_map/lt | solution.py:104
  38.7 2.9 %copy.17 = bf16[128,64,128]{2,0,1:T(8,128)(2,1)S(1)} copy(bf16[128,64,128]{2,1,0:T(8,128)(2,1)} %param.9) | data formatting | bytes 4194304 | tf_op args[0]
  41.8 4.6 %collective-permute-start.5 = (bf16[128,8,128]{2,0,1:T(8,128)(2,1)S(1)}, bf16[128,8,128]{2,0,1:T(8,128)(2,1)S(1)}, u32[]{:S(2)}, u32[]{:S(2)}) collective-permute-start(bf16[128,8,128]{2,0,1:T(8,128)(2,1)S(1)} %copy.12), channel_id=1, source_target_pairs={{0,3},{1,4},{2,5},{3,6},{4,7},{5,8},{6,9},{7,10},{8,11},{9,12},{10... | collective-permute-start | bytes 786440 | tf_op jit(solution)/shard_map/ppermute | solution.py:14
  46.4 1.0 constant_dynamic-update-slice_fusion.4
  47.4 3.5 %collective-permute-start.6 = (bf16[128,8,128]{2,0,1:T(8,128)(2,1)S(1)}, bf16[128,8,128]{2,0,1:T(8,128)(2,1)S(1)}, u32[]{:S(2)}, u32[]{:S(2)}) collective-permute-start(bf16[128,8,128]{2,0,1:T(8,128)(2,1)S(1)} %copy.12), channel_id=1, source_target_pairs={{0,2},{1,3},{2,4},{3,5},{4,6},{5,7},{6,8},{7,9},{8,10},{9,11},{10,... | collective-permute-start | bytes 786440 | tf_op jit(solution)/shard_map/ppermute | solution.py:14
  50.9 1.0 constant_dynamic-update-slice_fusion.3
  51.9 2.8 %collective-permute-start.7 = (bf16[128,8,128]{2,0,1:T(8,128)(2,1)S(1)}, bf16[128,8,128]{2,0,1:T(8,128)(2,1)S(1)}, u32[]{:S(2)}, u32[]{:S(2)}) collective-permute-start(bf16[128,8,128]{2,0,1:T(8,128)(2,1)S(1)} %copy.12), channel_id=1, source_target_pairs={{0,1},{1,2},{2,3},{3,4},{4,5},{5,6},{6,7},{7,8},{8,9},{9,10},{10,1... | collective-permute-start | bytes 786440 | tf_op jit(solution)/shard_map/ppermute | solution.py:14
  55.0 0.9 collective-permute-done.5
  55.9 5.0 %collective-permute-done.6 = bf16[128,8,128]{2,0,1:T(8,128)(2,1)S(1)} collective-permute-done((bf16[128,8,128]{2,0,1:T(8,128)(2,1)S(1)}, bf16[128,8,128]{2,0,1:T(8,128)(2,1)S(1)}, u32[]{:S(2)}, u32[]{:S(2)}) %collective-permute-start.6) | collective-permute-done | bytes 262176 | tf_op jit(solution)/shard_map/ppermute | solution.py:14
  61.0 3.0 %collective-permute-done.7 = bf16[128,8,128]{2,0,1:T(8,128)(2,1)S(1)} collective-permute-done((bf16[128,8,128]{2,0,1:T(8,128)(2,1)S(1)}, bf16[128,8,128]{2,0,1:T(8,128)(2,1)S(1)}, u32[]{:S(2)}, u32[]{:S(2)}) %collective-permute-start.7) | collective-permute-done | bytes 262176 | tf_op jit(solution)/shard_map/ppermute | solution.py:14
  64.2 1.0 copy-done.2
  65.2 46.6 %while.12 = (s32[]{:T(128)}, bf16[8,128,8,128]{1,3,2,0:T(8,128)(2,1)}, pred[128]{0:T(512)(128)(4,1)S(1)}, bf16[8,640,128]{1,2,0:T(8,128)(2,1)}, bf16[8,640,128]{...) while((s32[]{:T(128)}, ...), condition=%wide.region_3.4_spmd.clone, body=%wide.region_0.3_spmd.clone.sunk | while | flops 847531264 | bytes 2569213 | solution.py:91
  65.2 0.7 and_and_fusion.2
  65.9 2.1 %fusion.129 = f32[8,128]{1,0:T(8,128)S(1)} fusion(pred[128,640]{0,1:T(8,128)(4,1)S(1)} %and_and_fusion.2, bf16[8,128,8,128]{3,1,2,0:T(8,128)(2,1)S(1)} %get-tuple-element.244, s32[]{:T(128)} %get-tuple-element.226, bf16[8,640,128]{2,1,0:T(8,128)(2,1)} %get-tuple-element.243), kind=kOutput, calls=%fused_computation.84.clone.1 | convolution fusion | flops 339477120 | bytes 1021952 | tf_op jit(solution)/shard_map/while/body/eval_jaxpr/sub | solution.py:79
  68.0 3.0 %fusion.130 = bf16[8,128,8,128]{1,3,2,0:T(8,128)(2,1)} fusion(bf16[8,128,8,128]{1,3,2,0:T(8,128)(2,1)} %get-tuple-element.227, s32[]{:T(128)} %get-tuple-element.226, f32[128,8]{0,1:T(8,128)S(1)} %select_bitcast_fusion.2, pred[128]{0:T(512)(128)(4,1)S(1)} %get-tuple-element.241, bf16[8,640,128]{1,2,0:T(8,128)(2,1)} %get-tuple-element.242, ...), kind=kOutput, calls=%fused_computation.18.clone.1 | convolution fusion | flops 507643520 | bytes 1449472 | tf_op jit(solution)/shard_map/while/body/eval_jaxpr/gqk,kd->qgd/dot_general | solution.py:81
  71.0 0.7 and_and_fusion.2
  71.7 2.1 %fusion.129 = f32[8,128]{1,0:T(8,128)S(1)} fusion(pred[128,640]{0,1:T(8,128)(4,1)S(1)} %and_and_fusion.2, bf16[8,128,8,128]{3,1,2,0:T(8,128)(2,1)S(1)} %get-tuple-element.244, s32[]{:T(128)} %get-tuple-element.226, bf16[8,640,128]{2,1,0:T(8,128)(2,1)} %get-tuple-element.243), kind=kOutput, calls=%fused_computation.84.clone.1 | convolution fusion | flops 339477120 | bytes 1021952 | tf_op jit(solution)/shard_map/while/body/eval_jaxpr/sub | solution.py:79
  73.8 3.0 %fusion.130 = bf16[8,128,8,128]{1,3,2,0:T(8,128)(2,1)} fusion(bf16[8,128,8,128]{1,3,2,0:T(8,128)(2,1)} %get-tuple-element.227, s32[]{:T(128)} %get-tuple-element.226, f32[128,8]{0,1:T(8,128)S(1)} %select_bitcast_fusion.2, pred[128]{0:T(512)(128)(4,1)S(1)} %get-tuple-element.241, bf16[8,640,128]{1,2,0:T(8,128)(2,1)} %get-tuple-element.242, ...), kind=kOutput, calls=%fused_computation.18.clone.1 | convolution fusion | flops 507643520 | bytes 1449472 | tf_op jit(solution)/shard_map/while/body/eval_jaxpr/gqk,kd->qgd/dot_general | solution.py:81
  76.8 0.7 and_and_fusion.2
  77.5 2.1 %fusion.129 = f32[8,128]{1,0:T(8,128)S(1)} fusion(pred[128,640]{0,1:T(8,128)(4,1)S(1)} %and_and_fusion.2, bf16[8,128,8,128]{3,1,2,0:T(8,128)(2,1)S(1)} %get-tuple-element.244, s32[]{:T(128)} %get-tuple-element.226, bf16[8,640,128]{2,1,0:T(8,128)(2,1)} %get-tuple-element.243), kind=kOutput, calls=%fused_computation.84.clone.1 | convolution fusion | flops 339477120 | bytes 1021952 | tf_op jit(solution)/shard_map/while/body/eval_jaxpr/sub | solution.py:79
  79.6 3.0 %fusion.130 = bf16[8,128,8,128]{1,3,2,0:T(8,128)(2,1)} fusion(bf16[8,128,8,128]{1,3,2,0:T(8,128)(2,1)} %get-tuple-element.227, s32[]{:T(128)} %get-tuple-element.226, f32[128,8]{0,1:T(8,128)S(1)} %select_bitcast_fusion.2, pred[128]{0:T(512)(128)(4,1)S(1)} %get-tuple-element.241, bf16[8,640,128]{1,2,0:T(8,128)(2,1)} %get-tuple-element.242, ...), kind=kOutput, calls=%fused_computation.18.clone.1 | convolution fusion | flops 507643520 | bytes 1449472 | tf_op jit(solution)/shard_map/while/body/eval_jaxpr/gqk,kd->qgd/dot_general | solution.py:81
  82.7 0.7 and_and_fusion.2
  83.4 2.1 %fusion.129 = f32[8,128]{1,0:T(8,128)S(1)} fusion(pred[128,640]{0,1:T(8,128)(4,1)S(1)} %and_and_fusion.2, bf16[8,128,8,128]{3,1,2,0:T(8,128)(2,1)S(1)} %get-tuple-element.244, s32[]{:T(128)} %get-tuple-element.226, bf16[8,640,128]{2,1,0:T(8,128)(2,1)} %get-tuple-element.243), kind=kOutput, calls=%fused_computation.84.clone.1 | convolution fusion | flops 339477120 | bytes 1021952 | tf_op jit(solution)/shard_map/while/body/eval_jaxpr/sub | solution.py:79
  85.5 3.0 %fusion.130 = bf16[8,128,8,128]{1,3,2,0:T(8,128)(2,1)} fusion(bf16[8,128,8,128]{1,3,2,0:T(8,128)(2,1)} %get-tuple-element.227, s32[]{:T(128)} %get-tuple-element.226, f32[128,8]{0,1:T(8,128)S(1)} %select_bitcast_fusion.2, pred[128]{0:T(512)(128)(4,1)S(1)} %get-tuple-element.241, bf16[8,640,128]{1,2,0:T(8,128)(2,1)} %get-tuple-element.242, ...), kind=kOutput, calls=%fused_computation.18.clone.1 | convolution fusion | flops 507643520 | bytes 1449472 | tf_op jit(solution)/shard_map/while/body/eval_jaxpr/gqk,kd->qgd/dot_general | solution.py:81
  88.5 0.7 and_and_fusion.2
  89.2 2.1 %fusion.129 = f32[8,128]{1,0:T(8,128)S(1)} fusion(pred[128,640]{0,1:T(8,128)(4,1)S(1)} %and_and_fusion.2, bf16[8,128,8,128]{3,1,2,0:T(8,128)(2,1)S(1)} %get-tuple-element.244, s32[]{:T(128)} %get-tuple-element.226, bf16[8,640,128]{2,1,0:T(8,128)(2,1)} %get-tuple-element.243), kind=kOutput, calls=%fused_computation.84.clone.1 | convolution fusion | flops 339477120 | bytes 1021952 | tf_op jit(solution)/shard_map/while/body/eval_jaxpr/sub | solution.py:79
  91.3 3.0 %fusion.130 = bf16[8,128,8,128]{1,3,2,0:T(8,128)(2,1)} fusion(bf16[8,128,8,128]{1,3,2,0:T(8,128)(2,1)} %get-tuple-element.227, s32[]{:T(128)} %get-tuple-element.226, f32[128,8]{0,1:T(8,128)S(1)} %select_bitcast_fusion.2, pred[128]{0:T(512)(128)(4,1)S(1)} %get-tuple-element.241, bf16[8,640,128]{1,2,0:T(8,128)(2,1)} %get-tuple-element.242, ...), kind=kOutput, calls=%fused_computation.18.clone.1 | convolution fusion | flops 507643520 | bytes 1449472 | tf_op jit(solution)/shard_map/while/body/eval_jaxpr/gqk,kd->qgd/dot_general | solution.py:81
  94.3 0.7 and_and_fusion.2
  95.0 2.1 %fusion.129 = f32[8,128]{1,0:T(8,128)S(1)} fusion(pred[128,640]{0,1:T(8,128)(4,1)S(1)} %and_and_fusion.2, bf16[8,128,8,128]{3,1,2,0:T(8,128)(2,1)S(1)} %get-tuple-element.244, s32[]{:T(128)} %get-tuple-element.226, bf16[8,640,128]{2,1,0:T(8,128)(2,1)} %get-tuple-element.243), kind=kOutput, calls=%fused_computation.84.clone.1 | convolution fusion | flops 339477120 | bytes 1021952 | tf_op jit(solution)/shard_map/while/body/eval_jaxpr/sub | solution.py:79
  97.1 3.0 %fusion.130 = bf16[8,128,8,128]{1,3,2,0:T(8,128)(2,1)} fusion(bf16[8,128,8,128]{1,3,2,0:T(8,128)(2,1)} %get-tuple-element.227, s32[]{:T(128)} %get-tuple-element.226, f32[128,8]{0,1:T(8,128)S(1)} %select_bitcast_fusion.2, pred[128]{0:T(512)(128)(4,1)S(1)} %get-tuple-element.241, bf16[8,640,128]{1,2,0:T(8,128)(2,1)} %get-tuple-element.242, ...), kind=kOutput, calls=%fused_computation.18.clone.1 | convolution fusion | flops 507643520 | bytes 1449472 | tf_op jit(solution)/shard_map/while/body/eval_jaxpr/gqk,kd->qgd/dot_general | solution.py:81
  100.2 0.7 and_and_fusion.2
  100.8 2.1 %fusion.129 = f32[8,128]{1,0:T(8,128)S(1)} fusion(pred[128,640]{0,1:T(8,128)(4,1)S(1)} %and_and_fusion.2, bf16[8,128,8,128]{3,1,2,0:T(8,128)(2,1)S(1)} %get-tuple-element.244, s32[]{:T(128)} %get-tuple-element.226, bf16[8,640,128]{2,1,0:T(8,128)(2,1)} %get-tuple-element.243), kind=kOutput, calls=%fused_computation.84.clone.1 | convolution fusion | flops 339477120 | bytes 1021952 | tf_op jit(solution)/shard_map/while/body/eval_jaxpr/sub | solution.py:79
  102.9 3.0 %fusion.130 = bf16[8,128,8,128]{1,3,2,0:T(8,128)(2,1)} fusion(bf16[8,128,8,128]{1,3,2,0:T(8,128)(2,1)} %get-tuple-element.227, s32[]{:T(128)} %get-tuple-element.226, f32[128,8]{0,1:T(8,128)S(1)} %select_bitcast_fusion.2, pred[128]{0:T(512)(128)(4,1)S(1)} %get-tuple-element.241, bf16[8,640,128]{1,2,0:T(8,128)(2,1)} %get-tuple-element.242, ...), kind=kOutput, calls=%fused_computation.18.clone.1 | convolution fusion | flops 507643520 | bytes 1449472 | tf_op jit(solution)/shard_map/while/body/eval_jaxpr/gqk,kd->qgd/dot_general | solution.py:81
  106.0 0.7 and_and_fusion.2
  106.7 2.1 %fusion.129 = f32[8,128]{1,0:T(8,128)S(1)} fusion(pred[128,640]{0,1:T(8,128)(4,1)S(1)} %and_and_fusion.2, bf16[8,128,8,128]{3,1,2,0:T(8,128)(2,1)S(1)} %get-tuple-element.244, s32[]{:T(128)} %get-tuple-element.226, bf16[8,640,128]{2,1,0:T(8,128)(2,1)} %get-tuple-element.243), kind=kOutput, calls=%fused_computation.84.clone.1 | convolution fusion | flops 339477120 | bytes 1021952 | tf_op jit(solution)/shard_map/while/body/eval_jaxpr/sub | solution.py:79
  108.8 3.0 %fusion.130 = bf16[8,128,8,128]{1,3,2,0:T(8,128)(2,1)} fusion(bf16[8,128,8,128]{1,3,2,0:T(8,128)(2,1)} %get-tuple-element.227, s32[]{:T(128)} %get-tuple-element.226, f32[128,8]{0,1:T(8,128)S(1)} %select_bitcast_fusion.2, pred[128]{0:T(512)(128)(4,1)S(1)} %get-tuple-element.241, bf16[8,640,128]{1,2,0:T(8,128)(2,1)} %get-tuple-element.242, ...), kind=kOutput, calls=%fused_computation.18.clone.1 | convolution fusion | flops 507643520 | bytes 1449472 | tf_op jit(solution)/shard_map/while/body/eval_jaxpr/gqk,kd->qgd/dot_general | solution.py:81
  111.8 4.1 %copy.18 = bf16[128,8,8,128]{3,2,1,0:T(8,128)(2,1)} copy(bf16[128,8,8,128]{0,3,2,1:T(8,128)(2,1)} %bitcast.151) | data formatting | bytes 4194304 | tf_op jit(solution)/shard_map/transpose | solution.py:92
  (37 shorter events, 1.0 us)
Async XLA Ops:
  1.2 40.6 %collective-permute-start = (bf16[128,8,128]{0,2,1:T(8,128)(2,1)S(1)}, bf16[128,8,128]{0,2,1:T(8,128)(2,1)}, u32[]{:S(2)}, u32[]{:S(2)}) collective-permute-start(bf16[128,8,128]{0,2,1:T(8,128)(2,1)S(1)} %copy.7), channel_id=1, source_target_pairs={{0,4},{1,5},{2,6},{3,7},{4,8},{5,9},{6,10},{7,11},{8,12},{9,13},{1... | collective-permute-start | bytes 786440 | tf_op jit(solution)/shard_map/ppermute | solution.py:14
  4.6 42.7 %collective-permute-start.1 = (bf16[128,8,128]{0,2,1:T(8,128)(2,1)S(1)}, bf16[128,8,128]{0,2,1:T(8,128)(2,1)}, u32[]{:S(2)}, u32[]{:S(2)}) collective-permute-start(bf16[128,8,128]{0,2,1:T(8,128)(2,1)S(1)} %copy.7), channel_id=1, source_target_pairs={{0,3},{1,4},{2,5},{3,6},{4,7},{5,8},{6,9},{7,10},{8,11},{9,12},{10... | collective-permute-start | bytes 786440 | tf_op jit(solution)/shard_map/ppermute | solution.py:14
  9.3 42.6 %collective-permute-start.2 = (bf16[128,8,128]{0,2,1:T(8,128)(2,1)S(1)}, bf16[128,8,128]{0,2,1:T(8,128)(2,1)S(1)}, u32[]{:S(2)}, u32[]{:S(2)}) collective-permute-start(bf16[128,8,128]{0,2,1:T(8,128)(2,1)S(1)} %copy.7), channel_id=1, source_target_pairs={{0,2},{1,3},{2,4},{3,5},{4,6},{5,7},{6,8},{7,9},{8,10},{9,11},{10,... | collective-permute-start | bytes 786440 | tf_op jit(solution)/shard_map/ppermute | solution.py:14
  12.8 42.0 %collective-permute-start.3 = (bf16[128,8,128]{0,2,1:T(8,128)(2,1)S(1)}, bf16[128,8,128]{0,2,1:T(8,128)(2,1)S(1)}, u32[]{:S(2)}, u32[]{:S(2)}) collective-permute-start(bf16[128,8,128]{0,2,1:T(8,128)(2,1)S(1)} %copy.7), channel_id=1, source_target_pairs={{0,1},{1,2},{2,3},{3,4},{4,5},{5,6},{6,7},{7,8},{8,9},{9,10},{10,1... | collective-permute-start | bytes 786440 | tf_op jit(solution)/shard_map/ppermute | solution.py:14
  16.8 24.8 %all-to-all-start = ((s32[16,1,128]{2,1,0:T(1,128)}), s32[16,1,128]{2,1,0:T(1,128)S(1)}, u32[]{:S(2)}, u32[]{:S(2)}) async-start(s32[16,1,128]{2,1,0:T(1,128)} %broadcast_in_dim.79), calls=%async_computation | async-start | bytes 16384 | tf_op jit(solution)/shard_map/all_to_all | solution.py:25
  22.9 32.0 %collective-permute-start.4 = (bf16[128,8,128]{2,0,1:T(8,128)(2,1)S(1)}, bf16[128,8,128]{2,0,1:T(8,128)(2,1)S(1)}, u32[]{:S(2)}, u32[]{:S(2)}) collective-permute-start(bf16[128,8,128]{2,0,1:T(8,128)(2,1)S(1)} %copy.12), channel_id=1, source_target_pairs={{0,4},{1,5},{2,6},{3,7},{4,8},{5,9},{6,10},{7,11},{8,12},{9,13},{1... | collective-permute-start | bytes 786440 | tf_op jit(solution)/shard_map/ppermute | solution.py:14
  41.8 14.1 %collective-permute-start.5 = (bf16[128,8,128]{2,0,1:T(8,128)(2,1)S(1)}, bf16[128,8,128]{2,0,1:T(8,128)(2,1)S(1)}, u32[]{:S(2)}, u32[]{:S(2)}) collective-permute-start(bf16[128,8,128]{2,0,1:T(8,128)(2,1)S(1)} %copy.12), channel_id=1, source_target_pairs={{0,3},{1,4},{2,5},{3,6},{4,7},{5,8},{6,9},{7,10},{8,11},{9,12},{10... | collective-permute-start | bytes 786440 | tf_op jit(solution)/shard_map/ppermute | solution.py:14
  47.4 16.7 %copy-start = (bf16[128,8,128]{2,1,0:T(8,128)(2,1)S(1)}, bf16[128,8,128]{2,1,0:T(8,128)(2,1)}, u32[]{:S(2)}) copy-start(bf16[128,8,128]{2,1,0:T(8,128)(2,1)} %param.10) | copy-start | bytes 786436
  47.4 13.6 %collective-permute-start.6 = (bf16[128,8,128]{2,0,1:T(8,128)(2,1)S(1)}, bf16[128,8,128]{2,0,1:T(8,128)(2,1)S(1)}, u32[]{:S(2)}, u32[]{:S(2)}) collective-permute-start(bf16[128,8,128]{2,0,1:T(8,128)(2,1)S(1)} %copy.12), channel_id=1, source_target_pairs={{0,2},{1,3},{2,4},{3,5},{4,6},{5,7},{6,8},{7,9},{8,10},{9,11},{10,... | collective-permute-start | bytes 786440 | tf_op jit(solution)/shard_map/ppermute | solution.py:14
  51.9 12.1 %collective-permute-start.7 = (bf16[128,8,128]{2,0,1:T(8,128)(2,1)S(1)}, bf16[128,8,128]{2,0,1:T(8,128)(2,1)S(1)}, u32[]{:S(2)}, u32[]{:S(2)}) collective-permute-start(bf16[128,8,128]{2,0,1:T(8,128)(2,1)S(1)} %copy.12), channel_id=1, source_target_pairs={{0,1},{1,2},{2,3},{3,4},{4,5},{5,6},{6,7},{7,8},{8,9},{9,10},{10,1... | collective-permute-start | bytes 786440 | tf_op jit(solution)/shard_map/ppermute | solution.py:14
  54.9 9.2 %copy-start.1 = (bf16[640,8,128]{0,2,1:T(8,128)(2,1)}, bf16[640,8,128]{0,2,1:T(8,128)(2,1)S(1)}, u32[]{:S(2)}) copy-start(bf16[640,8,128]{0,2,1:T(8,128)(2,1)S(1)} %constant_dynamic-update-slice_fusion) | copy-start | bytes 3932164
  64.2 1.1 copy-start.2
where the time goes:
time: 117 us; the launch traced here: 116 us
  matrix products  40.9 us (35%)
  starting transfers between devices  33.7 us (29%)
  local copies, waits for them, and re-layouts  16.1 us (14%)
  other arithmetic  15.8 us (14%)
  waiting for transfers between devices  8.99 us (8%)
    ppermute x8, starting transfers between devices, from_behind(): return lax.ppermute(array, axis, pairs)  28.6 us
    dot_general x8, matrix products, one_group(): jnp.einsum('gqk,kd->qgd', weights.astype(jnp.bfloat16), value_group, pref...  24.2 us
    sub x8, matrix products, one_group(): weights = jnp.where(allowed[None], jnp.exp(scores - top), 0.0)  16.6 us
    ppermute x8, waiting for transfers between devices, from_behind(): return lax.ppermute(array, axis, pairs)  8.99 us
    unnamed x17, local copies, waits for them, and re-layouts  8.4 us
    lt x1, other arithmetic, local(): positions % shard_rows  5.55 us
    and x8, other arithmetic, window_attend(): (key_doc[None, :] == query_doc[:, None]) & (key_pos[None, :] <= query_pos...  5.48 us
    all_to_all x1, starting transfers between devices, sent_to_all(): lax.all_to_all(jnp.broadcast_to(array[None], (size, *array.shape)), axis,...  5.1 us
  transfers between devices with their start and end apart: 9, of which 3 were waited for; matrix products, arithmetic and copies ran while one was open for 17% of the time, Pallas kernels for 0%

commit v1 on v0

v1 whole, which is shorter than its diff:
```python
import functools
import math

import jax
import jax.numpy as jnp
from jax import lax
from jax.experimental import pallas as pl
from jax.experimental.pallas import tpu as pltpu
from jax.sharding import PartitionSpec as P

SPLIT = (4, 4)
ROWS = 512
BACK = (4, 3, 2, 1, 0)
MASKED = -1e30


def attend_kernel(place, counts, q_ref, *refs, scale):
    blocks = len(BACK)
    k_refs, v_refs, d_refs = refs[:blocks], refs[blocks : 2 * blocks], refs[2 * blocks : 3 * blocks]
    out_ref, bias, key_window, value_window = refs[-4:]
    shard, group, width = q_ref.shape
    window = blocks * shard
    me = place[0]

    @pl.when(pl.program_id(0) == 0)
    def _():
        own = d_refs[-1][0:1, :].astype(jnp.float32)
        query_doc = jnp.transpose(jnp.broadcast_to(own, (shard, shard)))
        column = lax.broadcasted_iota(jnp.int32, (shard, shard), 1)
        row = lax.broadcasted_iota(jnp.int32, (shard, shard), 0)
        for i, back in enumerate(BACK):
            live = jnp.where(me >= back, counts[jnp.maximum(me - back, 0)], 0)
            key_doc = jnp.broadcast_to(d_refs[i][0:1, :].astype(jnp.float32), (shard, shard))
            allowed = (key_doc == query_doc) & (column < live)
            if back == 0:
                allowed = allowed & (column <= row)
            here = jnp.where(allowed, 0.0, MASKED)
            bias[:, :, i * shard : (i + 1) * shard] = jnp.broadcast_to(
                here[:, None, :], (shard, group, shard)
            )

    for i in range(blocks):
        key_window[i * shard : (i + 1) * shard, :] = k_refs[i][...]
        value_window[i * shard : (i + 1) * shard, :] = v_refs[i][...]
    count = counts[me]
    tall = ROWS // group
    for start in range(0, shard, tall):
        q = q_ref[start : start + tall].reshape(ROWS, width)
        scores = lax.dot_general(
            q, key_window[...], (((1,), (1,)), ((), ())), preferred_element_type=jnp.float32
        )
        scores = scores + bias[start : start + tall].reshape(ROWS, window)
        top = jnp.max(scores, axis=1, keepdims=True)
        weights = jnp.exp2((scores - top) * scale)
        norm = jnp.sum(weights, axis=1, keepdims=True)
        mixed = jnp.dot(
            weights.astype(jnp.bfloat16), value_window[...], preferred_element_type=jnp.float32
        )
        position = lax.broadcasted_iota(jnp.int32, (ROWS, 1), 0) // group + start
        inverse = jnp.where(position < count, 1.0 / norm, 0.0)
        out_ref[start : start + tall] = (
            (mixed * inverse).astype(jnp.bfloat16).reshape(tall, group, width)
        )


def attend(place, counts, queries, parts, docs, first, heads, kv_heads, earlier):
    shard, query_heads, width = queries.shape
    group = query_heads // kv_heads
    blocks = len(BACK)
    doc_block = [d.shape[0] // 16 - 1 for d in docs]
    window = blocks * shard
    in_specs = [pl.BlockSpec(memory_space=pltpu.SMEM)] * 2
    in_specs += [pl.BlockSpec((shard, group, width), lambda g: (0, first + g, 0))]
    in_specs += [pl.BlockSpec((shard, width), lambda g: (g, 0))] * blocks
    in_specs += [pl.BlockSpec((shard, width), lambda g: (heads + g, 0))] * blocks
    in_specs += [pl.BlockSpec((16, width), lambda g, at=at: (at, 0)) for at in doc_block]
    operands = [place, counts, queries, *parts, *parts, *docs]
    aliases = {}
    if earlier is not None:
        in_specs.append(pl.BlockSpec(memory_space=pl.ANY))
        aliases = {len(operands): 0}
        operands.append(earlier)
    rows = shard * group * heads
    return pl.pallas_call(
        functools.partial(attend_kernel, scale=math.log2(math.e) / math.sqrt(width)),
        grid=(heads,),
        out_shape=jax.ShapeDtypeStruct(queries.shape, jnp.bfloat16),
        in_specs=in_specs,
        out_specs=pl.BlockSpec((shard, group, width), lambda g: (0, first + g, 0)),
        scratch_shapes=[
            pltpu.VMEM((shard, group, window), jnp.float32),
            pltpu.VMEM((window, width), jnp.bfloat16),
            pltpu.VMEM((window, width), jnp.bfloat16),
        ],
        input_output_aliases=aliases,
        compiler_params=pltpu.CompilerParams(vmem_limit_bytes=32 << 20),
        cost_estimate=pl.CostEstimate(
            flops=4 * rows * window * width,
            bytes_accessed=4 * rows * width + 4 * heads * window * width,
            transcendentals=rows * window,
        ),
        name="attend",
    )(*operands)


def row_permute(array, pairs):
    rows = lax.axis_size("seq") // 4
    return lax.ppermute(array, "seq", [(4 * r + i, 4 * r + j) for r in range(rows) for i, j in pairs])


def earlier_shards(own, x):
    size = lax.axis_size("seq")
    back4 = lax.ppermute(own, "seq", [(i, i + 4) for i in range(size - 4)])
    back1 = row_permute(jnp.where(x < 3, own, back4), [(0, 1), (1, 2), (2, 3), (3, 0)])
    back3 = row_permute(jnp.where(x < 1, own, back4), [(0, 3), (1, 0), (2, 1), (3, 2)])
    back2 = row_permute(jnp.where(x % 2 == 0, back1, back3), [(0, 1), (1, 0), (2, 3), (3, 2)])
    return [back4, back3, back2, back1, own]


def local(queries, keys, values, doc_ids, counts):
    shard, kv_heads, width = keys.shape
    device = lax.axis_index("seq")
    x = device % 4
    place = device.reshape(1)
    keys_by_head = jnp.transpose(keys, (1, 0, 2))
    values_by_head = jnp.transpose(values, (1, 0, 2))
    doc_rows = jnp.broadcast_to(doc_ids.astype(jnp.bfloat16)[None], (16, width))
    first = 0
    parts = []
    for i, heads in enumerate(SPLIT):
        pieces = [
            keys_by_head[first : first + heads].reshape(heads * shard, width),
            values_by_head[first : first + heads].reshape(heads * shard, width),
        ]
        if i == 0:
            pieces.append(doc_rows)
        parts.append(earlier_shards(jnp.concatenate(pieces), x))
        first += heads
    result = None
    first = 0
    for i, heads in enumerate(SPLIT):
        result = attend(
            place, counts, queries, parts[i], parts[0], first, heads, kv_heads, result
        )
        first += heads
    return result


def solution(mesh):
    in_specs = (
        P(("dp", "seq"), None, None),
        P(("dp", "seq"), None, None),
        P(("dp", "seq"), None, None),
        P(("dp", "seq")),
        P("dp"),
    )
    out_specs = P(("dp", "seq"), None, None)
    return jax.shard_map(local, mesh=mesh, in_specs=in_specs, out_specs=out_specs, check_vma=False)
```

time: 117 us -> 53.4 us (0.46)
  matrix products: 40.9 us -> 0 us
  starting transfers between devices: 33.7 us -> 14.7 us
  Pallas kernels: 0 us -> 16.9 us
  local copies, waits for them, and re-layouts: 16.1 us -> 3.08 us
  other arithmetic: 15.8 us -> 3.44 us
  waiting for transfers between devices: 8.99 us -> 14.9 us
    dot_general x8 -> x0, matrix products: 24.2 us -> none  [one_group(): jnp.einsum('gqk,kd->qgd', weights.astype(jnp.bfloat16), value_group, pref...]
    pallas_call x0 -> x2, Pallas kernels: none -> 16.9 us  [attend(): pl.pallas_call(functools.partial(attend_kernel, scale=math.log2(math.e) /...]
    sub x8 -> x0, matrix products: 16.6 us -> none  [one_group(): weights = jnp.where(allowed[None], jnp.exp(scores - top), 0.0)]
    ppermute x8, starting transfers between devices: 28.6 us -> 14.7 us  [the longest x6 7.93 us: row_permute(): lax.ppermute(array, 'seq', [(4 * r + i, 4 * r + j) for r in range(rows) f...]
    unnamed x17 -> x8, local copies, waits for them, and re-layouts: 8.4 us -> 0.68 us
    ppermute x8, waiting for transfers between devices: 8.99 us -> 14.9 us  [the longest x6 11.7 us: row_permute(): lax.ppermute(array, 'seq', [(4 * r + i, 4 * r + j) for r in range(rows) f...]
    lt x1 -> x0, other arithmetic: 5.55 us -> none  [local(): positions % shard_rows]
    and x8 -> x0, other arithmetic: 5.48 us -> none  [window_attend(): (key_doc[None, :] == query_doc[:, None]) & (key_pos[None, :] <= query_pos...]
  transfers between devices with their start and end apart: 9 -> 8, of which waited for: 3 -> 5; matrix products, arithmetic and copies ran while one was open for 17% -> 5% of each run, Pallas kernels for 0% -> 16%
where the time goes in v1:
time: 53.4 us; the launch traced here: 53.1 us
  Pallas kernels  16.9 us (32%)
  waiting for transfers between devices  14.9 us (28%)
  starting transfers between devices  14.7 us (28%)
  other arithmetic  3.44 us (6%)
  local copies, waits for them, and re-layouts  3.08 us (6%)
    pallas_call x2, Pallas kernels, attend(): pl.pallas_call(functools.partial(attend_kernel, scale=math.log2(math.e) /...  16.9 us
    ppermute x6, waiting for transfers between devices, row_permute(): lax.ppermute(array, 'seq', [(4 * r + i, 4 * r + j) for r in range(rows) f...  11.7 us
    ppermute x6, starting transfers between devices, row_permute(): lax.ppermute(array, 'seq', [(4 * r + i, 4 * r + j) for r in range(rows) f...  7.93 us
    ppermute x2, starting transfers between devices, earlier_shards(): back4 = lax.ppermute(own, 'seq', [(i, i + 4) for i in range(size - 4)])  6.79 us
    ppermute x2, waiting for transfers between devices, earlier_shards(): back4 = lax.ppermute(own, 'seq', [(i, i + 4) for i in range(size - 4)])  3.2 us
    select_n x2, other arithmetic, earlier_shards(): jnp.where(x < 3, own, back4)  1.99 us
    slice x3, local copies, waits for them, and re-layouts, local(): keys_by_head[first:first + heads].reshape(heads * shard, width)  1.21 us
    slice x3, local copies, waits for them, and re-layouts, local(): values_by_head[first:first + heads].reshape(heads * shard, width)  1.18 us
  transfers between devices with their start and end apart: 8, of which 5 were waited for; matrix products, arithmetic and copies ran while one was open for 5% of the time, Pallas kernels for 16%

profile of v1, /device:TPU:232, one launch (start us, length us, event | category | flops | bytes accessed | tf_op | source)
XLA Modules:
  0.0 53.1 jit_solution(17664980318783690489)
XLA Ops:
  0.0 0.7 %convert_element_type.3 = bf16[128]{0:T(256)(128)(2,1)S(1)} convert(s32[128]{0:T(128)} %param.8) | non-fusion elementwise | flops 128 | bytes 768 | tf_op jit(solution)/shard_map/convert_element_type | solution.py:127
  0.7 1.2 %fusion = (bf16[4,128,128]{2,0,1:T(4,128)(2,1)S(1)}, bf16[4,128,128]{2,0,1:T(4,128)(2,1)S(1)}) fusion(bf16[8,128,128]{2,0,1:T(8,128)(2,1)} %bitcast.15), kind=kLoop, calls=%fused_computation.8 | loop fusion | bytes 524288 | tf_op jit(solution)/shard_map/slice | solution.py:132
  1.9 1.1 %fusion.1 = (bf16[4,128,128]{2,0,1:T(4,128)(2,1)S(1)}, bf16[4,128,128]{2,0,1:T(4,128)(2,1)S(1)}) fusion(bf16[8,128,128]{2,0,1:T(8,128)(2,1)} %bitcast.16), kind=kLoop, calls=%fused_computation.9 | loop fusion | bytes 524288 | tf_op jit(solution)/shard_map/slice | solution.py:133
  3.1 3.5 %collective-permute-start.4 = (bf16[1040,128]{1,0:T(8,128)(2,1)S(1)}, bf16[1040,128]{1,0:T(8,128)(2,1)S(1)}, u32[]{:S(2)}, u32[]{:S(2)}) collective-permute-start(bf16[1040,128]{1,0:T(8,128)(2,1)S(1)} %pad_maximum_fusion.refs_4_.refs_9_.refs_14_), channel_id=1, source_target_pairs={{0,4},{1,5},{2,6},{3,7},{4,8},{5,9},{6,10},{7,11},{8,12},{9,13},{1... | collective-permute-start | bytes 798728 | tf_op jit(solution)/shard_map/ppermute | solution.py:113
  6.6 0.0 copy-start.2
  6.6 0.0 copy-start.3
  6.6 0.6 %copy-done.2 = bf16[4,128,128]{2,1,0:T(8,128)(2,1)} copy-done((bf16[4,128,128]{2,1,0:T(8,128)(2,1)}, bf16[4,128,128]{2,1,0:T(8,128)(2,1)S(1)}, u32[]{:S(2)}) %copy-start.2) | copy-done | bytes 131096
  7.2 0.1 copy-done.3
  7.3 0.0 copy-start
  7.3 0.0 copy-start.1
  7.3 0.7 %pad_maximum_fusion.1.refs_4_.refs_9_ = bf16[1024,128]{1,0:T(8,128)(2,1)} fusion(bf16[512,128]{1,0:T(8,128)(2,1)S(1)} %bitcast.9, bf16[512,128]{1,0:T(8,128)(2,1)S(1)} %bitcast.7), kind=kLoop, calls=%fused_computation.4 | loop fusion | flops 524288 | bytes 524288 | tf_op jit(solution)/shard_map/concatenate | solution.py:137
  8.0 3.3 %collective-permute-start = (bf16[1024,128]{1,0:T(8,128)(2,1)}, bf16[1024,128]{1,0:T(8,128)(2,1)S(1)}, u32[]{:S(2)}, u32[]{:S(2)}) collective-permute-start(bf16[1024,128]{1,0:T(8,128)(2,1)} %pad_maximum_fusion.1.refs_4_.refs_9_), channel_id=1, source_target_pairs={{0,4},{1,5},{2,6},{3,7},{4,8},{5,9},{6,10},{7,11},{8,12},{9,13},{1... | collective-permute-start | bytes 786440 | tf_op jit(solution)/shard_map/ppermute | solution.py:113
  11.4 2.4 %collective-permute-done.4.refs_0_.refs_5_.refs_10_ = bf16[1040,128]{1,0:T(8,128)(2,1)S(1)} collective-permute-done((bf16[1040,128]{1,0:T(8,128)(2,1)S(1)}, bf16[1040,128]{1,0:T(8,128)(2,1)S(1)}, u32[]{:S(2)}, u32[]{:S(2)}) %collective-permute-start.4) | collective-permute-done | bytes 266272 | tf_op jit(solution)/shard_map/ppermute | solution.py:113
  13.8 0.9 %broadcast_select_fusion = (bf16[1040,128]{1,0:T(8,128)(2,1)}, bf16[1040,128]{1,0:T(8,128)(2,1)}) fusion(bf16[1040,128]{1,0:T(8,128)(2,1)S(1)} %collective-permute-done.4.refs_0_.refs_5_.refs_10_, pred[]{:T(512)S(6)} %lt.23, bf16[16,128]{1,0:T(8,128)(2,1)S(1)} %broadcast_in_dim.2, bf16[512,128]{1,0:T(8,128)(2,1)S(1)} %bitcast.14, ...), kind=kLoop, calls=%fused_computation.1 | loop fusion | flops 1064960 | bytes 1064962 | tf_op jit(solution)/shard_map/jit(_where)/select_n | solution.py:114
  14.7 1.5 %collective-permute-start.6 = (bf16[1040,128]{1,0:T(8,128)(2,1)}, bf16[1040,128]{1,0:T(8,128)(2,1)S(1)}, u32[]{:S(2)}, u32[]{:S(2)}) collective-permute-start(bf16[1040,128]{1,0:T(8,128)(2,1)} %get-tuple-element.5), channel_id=1, source_target_pairs={{0,1},{1,2},{2,3},{3,0},{4,5},{5,6},{6,7},{7,4},{8,9},{9,10},{10,1... | collective-permute-start | bytes 798728 | tf_op jit(solution)/shard_map/ppermute | solution.py:108
  16.2 1.7 %collective-permute-start.5 = (bf16[1040,128]{1,0:T(8,128)(2,1)}, bf16[1040,128]{1,0:T(8,128)(2,1)S(1)}, u32[]{:S(2)}, u32[]{:S(2)}) collective-permute-start(bf16[1040,128]{1,0:T(8,128)(2,1)} %get-tuple-element.6), channel_id=1, source_target_pairs={{0,3},{1,0},{2,1},{3,2},{4,7},{5,4},{6,5},{7,6},{8,11},{9,8},{10,9... | collective-permute-start | bytes 798728 | tf_op jit(solution)/shard_map/ppermute | solution.py:108
  17.9 0.8 %collective-permute-done.refs_0_.refs_5_ = bf16[1024,128]{1,0:T(8,128)(2,1)S(1)} collective-permute-done((bf16[1024,128]{1,0:T(8,128)(2,1)}, bf16[1024,128]{1,0:T(8,128)(2,1)S(1)}, u32[]{:S(2)}, u32[]{:S(2)}) %collective-permute-start) | collective-permute-done | bytes 262176 | tf_op jit(solution)/shard_map/ppermute | solution.py:113
  18.7 1.1 %broadcast_select_fusion.3 = (bf16[1024,128]{1,0:T(8,128)(2,1)S(1)}, bf16[1024,128]{1,0:T(8,128)(2,1)S(1)}) fusion(bf16[1024,128]{1,0:T(8,128)(2,1)S(1)} %collective-permute-done.refs_0_.refs_5_, pred[]{:T(512)S(6)} %lt.23, bf16[512,128]{1,0:T(8,128)(2,1)} %bitcast.10, bf16[512,128]{1,0:T(8,128)(2,1)} %bitcast.8, pred[]{:T(512)S(6)} %lt.21), kind=kLoop, calls=%fused_computation.5 | loop fusion | flops 786432 | bytes 1048578 | tf_op jit(solution)/shard_map/jit(_where)/select_n | solution.py:114
  19.8 1.6 %collective-permute-start.2 = (bf16[1024,128]{1,0:T(8,128)(2,1)S(1)}, bf16[1024,128]{1,0:T(8,128)(2,1)S(1)}, u32[]{:S(2)}, u32[]{:S(2)}) collective-permute-start(bf16[1024,128]{1,0:T(8,128)(2,1)S(1)} %get-tuple-element.7), channel_id=1, source_target_pairs={{0,1},{1,2},{2,3},{3,0},{4,5},{5,6},{6,7},{7,4},{8,9},{9,10},{10,1... | collective-permute-start | bytes 786440 | tf_op jit(solution)/shard_map/ppermute | solution.py:108
  21.4 1.7 %collective-permute-start.1 = (bf16[1024,128]{1,0:T(8,128)(2,1)S(1)}, bf16[1024,128]{1,0:T(8,128)(2,1)S(1)}, u32[]{:S(2)}, u32[]{:S(2)}) collective-permute-start(bf16[1024,128]{1,0:T(8,128)(2,1)S(1)} %get-tuple-element.8), channel_id=1, source_target_pairs={{0,3},{1,0},{2,1},{3,2},{4,7},{5,4},{6,5},{7,6},{8,11},{9,8},{10,9... | collective-permute-start | bytes 786440 | tf_op jit(solution)/shard_map/ppermute | solution.py:108
  23.1 0.0 collective-permute-done.6.refs_3_.refs_8_.refs_13_
  23.1 0.0 collective-permute-done.5.refs_1_.refs_6_.refs_11_
  23.2 1.3 %collective-permute-start.7 = (bf16[1040,128]{1,0:T(8,128)(2,1)S(1)}, bf16[1040,128]{1,0:T(8,128)(2,1)S(1)}, u32[]{:S(2)}, u32[]{:S(2)}) collective-permute-start(bf16[1040,128]{1,0:T(8,128)(2,1)S(1)} %broadcast_select_fusion.1), channel_id=1, source_target_pairs={{0,1},{1,0},{2,3},{3,2},{4,5},{5,4},{6,7},{7,6},{8,9},{9,8},{10,11... | collective-permute-start | bytes 798728 | tf_op jit(solution)/shard_map/ppermute | solution.py:108
  24.4 4.2 %collective-permute-done.2.refs_3_.refs_8_ = bf16[1024,128]{1,0:T(8,128)(2,1)S(1)} collective-permute-done((bf16[1024,128]{1,0:T(8,128)(2,1)S(1)}, bf16[1024,128]{1,0:T(8,128)(2,1)S(1)}, u32[]{:S(2)}, u32[]{:S(2)}) %collective-permute-start.2) | collective-permute-done | bytes 262176 | tf_op jit(solution)/shard_map/ppermute | solution.py:108
  28.7 1.8 %collective-permute-done.1.refs_1_.refs_6_ = bf16[1024,128]{1,0:T(8,128)(2,1)S(1)} collective-permute-done((bf16[1024,128]{1,0:T(8,128)(2,1)S(1)}, bf16[1024,128]{1,0:T(8,128)(2,1)S(1)}, u32[]{:S(2)}, u32[]{:S(2)}) %collective-permute-start.1) | collective-permute-done | bytes 262176 | tf_op jit(solution)/shard_map/ppermute | solution.py:108
  30.6 0.1 collective-permute-start.3
  30.7 5.6 %collective-permute-done.7.refs_2_.refs_7_.refs_12_ = bf16[1040,128]{1,0:T(8,128)(2,1)S(1)} collective-permute-done((bf16[1040,128]{1,0:T(8,128)(2,1)S(1)}, bf16[1040,128]{1,0:T(8,128)(2,1)S(1)}, u32[]{:S(2)}, u32[]{:S(2)}) %collective-permute-start.7) | collective-permute-done | bytes 266272 | tf_op jit(solution)/shard_map/ppermute | solution.py:108
  36.2 0.0 copy-done
  36.2 0.0 copy-done.1
  36.2 8.3 %attend.2.refs_15_ = bf16[128,64,128]{2,1,0:T(8,128)(2,1)} custom-call(s32[1]{0:T(128)} %bitcast.place, s32[16]{0:T(128)S(1)} %copy-done.1, bf16[128,64,128]{2,1,0:T(8,128)(2,1)S(1)} %copy-done, bf16[1040,128]{1,0:T(8,128)(2,1)S(1)} %collective-permute-done.4.refs_0_.refs_5_.refs_10_, bf16[1040,128]{1,0:T(8,128)(2,1)S(1)} %collective-permute-done.5.refs_1_.refs_6_.refs_11_, ...), custom_call_target="tpu_custom_call" | custom-call | flops 1342177280 | bytes 3407872 | tf_op jit(solution)/shard_map/attend/pallas_call | solution.py:84
  44.5 0.0 collective-permute-done.3.refs_2_.refs_7_
  44.5 8.6 %attend.3 = bf16[128,64,128]{2,1,0:T(8,128)(2,1)} custom-call(s32[1]{0:T(128)} %bitcast.place, s32[16]{0:T(128)S(1)} %copy-done.1, bf16[128,64,128]{2,1,0:T(8,128)(2,1)S(1)} %copy-done, bf16[1024,128]{1,0:T(8,128)(2,1)S(1)} %collective-permute-done.refs_0_.refs_5_, ...), custom_call_target="tpu_custom_call", output_to_operand_aliasing={{}: (18, {})} | custom-call | flops 1342177280 | bytes 3407872 | tf_op jit(solution)/shard_map/attend/pallas_call | solution.py:84
  (8 shorter events, 0.2 us)
Async XLA Ops:
  3.1 10.7 %collective-permute-start.4 = (bf16[1040,128]{1,0:T(8,128)(2,1)S(1)}, bf16[1040,128]{1,0:T(8,128)(2,1)S(1)}, u32[]{:S(2)}, u32[]{:S(2)}) collective-permute-start(bf16[1040,128]{1,0:T(8,128)(2,1)S(1)} %pad_maximum_fusion.refs_4_.refs_9_.refs_14_), channel_id=1, source_target_pairs={{0,4},{1,5},{2,6},{3,7},{4,8},{5,9},{6,10},{7,11},{8,12},{9,13},{1... | collective-permute-start | bytes 798728 | tf_op jit(solution)/shard_map/ppermute | solution.py:113
  6.6 0.7 %copy-start.2 = (bf16[4,128,128]{2,1,0:T(8,128)(2,1)}, bf16[4,128,128]{2,1,0:T(8,128)(2,1)S(1)}, u32[]{:S(2)}) copy-start(bf16[4,128,128]{2,1,0:T(8,128)(2,1)S(1)} %copy.7) | copy-start | bytes 393220
  6.6 0.7 %copy-start.3 = (bf16[4,128,128]{2,1,0:T(8,128)(2,1)}, bf16[4,128,128]{2,1,0:T(8,128)(2,1)S(1)}, u32[]{:S(2)}) copy-start(bf16[4,128,128]{2,1,0:T(8,128)(2,1)S(1)} %copy.8) | copy-start | bytes 393220
  7.3 28.9 %copy-start = (bf16[128,64,128]{2,1,0:T(8,128)(2,1)S(1)}, bf16[128,64,128]{2,1,0:T(8,128)(2,1)}, u32[]{:S(2)}) copy-start(bf16[128,64,128]{2,1,0:T(8,128)(2,1)} %q_ref.3) | copy-start | bytes 6291460
  7.3 28.9 %copy-start.1 = (s32[16]{0:T(128)S(1)}, s32[16]{0:T(128)}, u32[]{:S(2)}) copy-start(s32[16]{0:T(128)} %counts.3) | copy-start | bytes 196
  8.0 10.7 %collective-permute-start = (bf16[1024,128]{1,0:T(8,128)(2,1)}, bf16[1024,128]{1,0:T(8,128)(2,1)S(1)}, u32[]{:S(2)}, u32[]{:S(2)}) collective-permute-start(bf16[1024,128]{1,0:T(8,128)(2,1)} %pad_maximum_fusion.1.refs_4_.refs_9_), channel_id=1, source_target_pairs={{0,4},{1,5},{2,6},{3,7},{4,8},{5,9},{6,10},{7,11},{8,12},{9,13},{1... | collective-permute-start | bytes 786440 | tf_op jit(solution)/shard_map/ppermute | solution.py:113
  14.7 8.4 %collective-permute-start.6 = (bf16[1040,128]{1,0:T(8,128)(2,1)}, bf16[1040,128]{1,0:T(8,128)(2,1)S(1)}, u32[]{:S(2)}, u32[]{:S(2)}) collective-permute-start(bf16[1040,128]{1,0:T(8,128)(2,1)} %get-tuple-element.5), channel_id=1, source_target_pairs={{0,1},{1,2},{2,3},{3,0},{4,5},{5,6},{6,7},{7,4},{8,9},{9,10},{10,1... | collective-permute-start | bytes 798728 | tf_op jit(solution)/shard_map/ppermute | solution.py:108
  16.2 6.9 %collective-permute-start.5 = (bf16[1040,128]{1,0:T(8,128)(2,1)}, bf16[1040,128]{1,0:T(8,128)(2,1)S(1)}, u32[]{:S(2)}, u32[]{:S(2)}) collective-permute-start(bf16[1040,128]{1,0:T(8,128)(2,1)} %get-tuple-element.6), channel_id=1, source_target_pairs={{0,3},{1,0},{2,1},{3,2},{4,7},{5,4},{6,5},{7,6},{8,11},{9,8},{10,9... | collective-permute-start | bytes 798728 | tf_op jit(solution)/shard_map/ppermute | solution.py:108
  19.8 8.9 %collective-permute-start.2 = (bf16[1024,128]{1,0:T(8,128)(2,1)S(1)}, bf16[1024,128]{1,0:T(8,128)(2,1)S(1)}, u32[]{:S(2)}, u32[]{:S(2)}) collective-permute-start(bf16[1024,128]{1,0:T(8,128)(2,1)S(1)} %get-tuple-element.7), channel_id=1, source_target_pairs={{0,1},{1,2},{2,3},{3,0},{4,5},{5,6},{6,7},{7,4},{8,9},{9,10},{10,1... | collective-permute-start | bytes 786440 | tf_op jit(solution)/shard_map/ppermute | solution.py:108
  21.4 9.2 %collective-permute-start.1 = (bf16[1024,128]{1,0:T(8,128)(2,1)S(1)}, bf16[1024,128]{1,0:T(8,128)(2,1)S(1)}, u32[]{:S(2)}, u32[]{:S(2)}) collective-permute-start(bf16[1024,128]{1,0:T(8,128)(2,1)S(1)} %get-tuple-element.8), channel_id=1, source_target_pairs={{0,3},{1,0},{2,1},{3,2},{4,7},{5,4},{6,5},{7,6},{8,11},{9,8},{10,9... | collective-permute-start | bytes 786440 | tf_op jit(solution)/shard_map/ppermute | solution.py:108
  23.2 13.1 %collective-permute-start.7 = (bf16[1040,128]{1,0:T(8,128)(2,1)S(1)}, bf16[1040,128]{1,0:T(8,128)(2,1)S(1)}, u32[]{:S(2)}, u32[]{:S(2)}) collective-permute-start(bf16[1040,128]{1,0:T(8,128)(2,1)S(1)} %broadcast_select_fusion.1), channel_id=1, source_target_pairs={{0,1},{1,0},{2,3},{3,2},{4,5},{5,4},{6,7},{7,6},{8,9},{9,8},{10,11... | collective-permute-start | bytes 798728 | tf_op jit(solution)/shard_map/ppermute | solution.py:108
  30.6 14.0 %collective-permute-start.3 = (bf16[1024,128]{1,0:T(8,128)(2,1)S(1)}, bf16[1024,128]{1,0:T(8,128)(2,1)S(1)}, u32[]{:S(2)}, u32[]{:S(2)}) collective-permute-start(bf16[1024,128]{1,0:T(8,128)(2,1)S(1)} %broadcast_select_fusion.4), channel_id=1, source_target_pairs={{0,1},{1,0},{2,3},{3,2},{4,5},{5,4},{6,7},{7,6},{8,9},{9,8},{10,11... | collective-permute-start | bytes 786440 | tf_op jit(solution)/shard_map/ppermute | solution.py:108

commit v2 on v1

v2 whole, which is shorter than its diff:
```python
import functools
import math

import jax
import jax.numpy as jnp
from jax import lax
from jax.experimental import pallas as pl
from jax.experimental.pallas import tpu as pltpu
from jax.sharding import PartitionSpec as P


SPLIT = (2, 3, 3)
ROWS = 512
GROUP = 8
BACK = (4, 3, 2, 1, 0)
MASKED = -1e30


def pack_kernel(docs_hbm, keys_hbm, values_hbm, *refs):
    outs, (docs, keys, values, arrived) = refs[: len(SPLIT)], refs[len(SPLIT) :]
    shard, _, width = keys.shape
    sources = (keys_hbm, values_hbm, docs_hbm)
    copies = [
        pltpu.make_async_copy(source, target, arrived.at[i])
        for i, (source, target) in enumerate(zip(sources, (keys, values, docs)))
    ]
    for copy in copies:
        copy.start()
    for which, ref in ((0, keys), (1, values)):
        copies[which].wait()
        by_head = jnp.swapaxes(ref[...].astype(jnp.float32), 0, 1).astype(jnp.bfloat16)
        first = 0
        for out, heads in zip(outs, SPLIT):
            out[which * heads * shard : (which + 1) * heads * shard, :] = by_head[
                first : first + heads
            ].reshape(heads * shard, width)
            first += heads
    copies[2].wait()
    outs[0][2 * SPLIT[0] * shard :, :] = jnp.broadcast_to(
        docs[...].astype(jnp.float32), (16, width)
    ).astype(jnp.bfloat16)


def pack(doc_ids, keys, values):
    shard, _, width = keys.shape
    rows = [2 * heads * shard + (16 if i == 0 else 0) for i, heads in enumerate(SPLIT)]
    return pl.pallas_call(
        pack_kernel,
        out_shape=[jax.ShapeDtypeStruct((r, width), jnp.bfloat16) for r in rows],
        in_specs=[pl.BlockSpec(memory_space=pltpu.HBM)] * 3,
        out_specs=[pl.BlockSpec(memory_space=pltpu.VMEM)] * len(SPLIT),
        scratch_shapes=[
            pltpu.VMEM((1, width), jnp.int32),
            pltpu.VMEM(keys.shape, keys.dtype),
            pltpu.VMEM(values.shape, values.dtype),
            pltpu.SemaphoreType.DMA((3,)),
        ],
        compiler_params=pltpu.CompilerParams(vmem_limit_bytes=8 << 20),
        name="pack",
    )(
        *[
            pltpu.with_memory_space_constraint(a, pltpu.HBM)
            for a in (doc_ids.reshape(1, width), keys, values)
        ]
    )


def fill_mask(place, counts, docs, mask, shard):
    me = place[0]
    query_doc = jnp.broadcast_to(docs[-1].astype(jnp.float32), (shard, shard))
    query = lax.broadcasted_iota(jnp.int32, (shard, shard), 1)
    key = lax.broadcasted_iota(jnp.int32, (shard, shard), 0)
    for i, back in enumerate(BACK):
        live = jnp.where(me >= back, counts[jnp.maximum(me - back, 0)], 0)
        key_doc = jnp.transpose(jnp.broadcast_to(docs[i].astype(jnp.float32), (shard, shard)))
        allowed = (key_doc == query_doc) & (key < live)
        if back == 0:
            allowed = allowed & (key <= query)
        mask[i * shard : (i + 1) * shard, :] = jnp.where(allowed, 0.0, MASKED).astype(jnp.bfloat16)


def attend_kernel(place, counts, q_ref, *refs, scale, first, heads, makes_mask):
    blocks = len(BACK)
    parts, refs = refs[:blocks], refs[blocks:]
    shard, _, width = q_ref.shape
    group = GROUP
    if makes_mask:
        result, mask, *refs = refs
        at = 2 * heads * shard
        fill_mask(place, counts, [p[at : at + 1, :] for p in parts], mask, shard)
    else:
        mask, _, result, *refs = refs
    select, key_window, value_window, mixed_heads, sent = refs
    position = lax.broadcasted_iota(jnp.int32, (shard * group, shard), 0) // group
    column = lax.broadcasted_iota(jnp.int32, (shard * group, shard), 1)
    select[...] = jnp.where(position == column, 1.0, 0.0).astype(jnp.bfloat16)
    for j in range(heads):
        key_window[j, :, width:] = mask[...]
        for i in range(blocks):
            at = slice(i * shard, (i + 1) * shard)
            key_window[j, at, :width] = parts[i][j * shard : (j + 1) * shard, :]
            value_window[j, at, :] = parts[i][(heads + j) * shard : (heads + j + 1) * shard, :]
    count = counts[place[0]]
    tall = ROWS // group

    def score(j, c):
        at = (first + j) * group
        q = q_ref[c * tall : (c + 1) * tall, at : at + group].reshape(ROWS, width)
        q = jnp.concatenate([q, select[c * ROWS : (c + 1) * ROWS, :]], axis=1)
        return lax.dot_general(
            q, key_window[j], (((1,), (1,)), ((), ())), preferred_element_type=jnp.float32
        )

    def soften(scores):
        top = jnp.max(scores, axis=1, keepdims=True)
        weights = jnp.exp2((scores - top) * scale)
        return weights.astype(jnp.bfloat16), jnp.sum(weights, axis=1, keepdims=True)

    def leave(j):
        at = (first + j) * group
        return pltpu.make_async_copy(
            mixed_heads.at[j], result.at[:, at : at + group, :], sent.at[j]
        )

    def mix(j, c, weights, norm):
        mixed = jnp.dot(weights, value_window[j], preferred_element_type=jnp.float32)
        position = lax.broadcasted_iota(jnp.int32, (ROWS, 1), 0) // group + c * tall
        inverse = jnp.where(position < count, 1.0 / norm, 0.0)
        mixed_heads[j, c * tall : (c + 1) * tall] = (
            (mixed * inverse).astype(jnp.bfloat16).reshape(tall, group, width)
        )
        if (c + 1) * tall == shard:
            leave(j).start()

    work = [(j, c) for j in range(heads) for c in range(shard // tall)]
    scores = score(*work[0])
    waiting = None
    for i, (j, c) in enumerate(work):
        after = score(*work[i + 1]) if i + 1 < len(work) else None
        weights, norm = soften(scores)
        if waiting is not None:
            mix(*waiting)
        waiting = (j, c, weights, norm)
        scores = after
    mix(*waiting)
    for j in range(heads):
        leave(j).wait()


def attend(place, counts, queries, parts, first, heads, before):
    shard, _, width = queries.shape
    window = len(BACK) * shard
    vmem = pl.BlockSpec(memory_space=pltpu.VMEM)
    in_specs = [pl.BlockSpec(memory_space=pltpu.SMEM)] * 2 + [vmem] * (1 + len(BACK))
    operands = [place, counts, queries, *parts]
    out_shape = [jax.ShapeDtypeStruct(queries.shape, jnp.bfloat16)]
    out_specs = [pl.BlockSpec(memory_space=pltpu.HBM)]
    aliases = {}
    if before is None:
        out_shape.append(jax.ShapeDtypeStruct((window, shard), jnp.bfloat16))
        out_specs.append(vmem)
    else:
        result, mask = before
        in_specs += [vmem, pl.BlockSpec(memory_space=pltpu.HBM)]
        aliases = {len(operands) + 1: 0}
        operands += [mask, result]
    rows = shard * GROUP * heads
    out = pl.pallas_call(
        functools.partial(
            attend_kernel,
            scale=math.log2(math.e) / math.sqrt(width),
            first=first,
            heads=heads,
            makes_mask=before is None,
        ),
        out_shape=out_shape,
        in_specs=in_specs,
        out_specs=out_specs,
        scratch_shapes=[
            pltpu.VMEM((shard * GROUP, shard), jnp.bfloat16),
            pltpu.VMEM((heads, window, 2 * width), jnp.bfloat16),
            pltpu.VMEM((heads, window, width), jnp.bfloat16),
            pltpu.VMEM((heads, shard, GROUP, width), jnp.bfloat16),
            pltpu.SemaphoreType.DMA((heads,)),
        ],
        input_output_aliases=aliases,
        compiler_params=pltpu.CompilerParams(vmem_limit_bytes=32 << 20),
        cost_estimate=pl.CostEstimate(
            flops=4 * rows * window * width,
            bytes_accessed=4 * rows * width + 4 * heads * window * width,
            transcendentals=rows * window,
        ),
        name="attend",
    )(*operands)
    return out if before is None else [out[0], mask]


def row_permute(array, pairs):
    rows = lax.axis_size("seq") // 4
    return lax.ppermute(array, "seq", [(4 * r + i, 4 * r + j) for r in range(rows) for i, j in pairs])


def earlier_shards(own, x):
    size = lax.axis_size("seq")
    back4 = lax.ppermute(own, "seq", [(i, i + 4) for i in range(size - 4)])
    back1 = row_permute(jnp.where(x < 3, own, back4), [(0, 1), (1, 2), (2, 3), (3, 0)])
    back3 = row_permute(jnp.where(x < 1, own, back4), [(0, 3), (1, 0), (2, 1), (3, 2)])
    back2 = row_permute(
        jnp.where(x % 2 == 0, back1, back3), [(0, 1), (1, 0), (2, 3), (3, 2)]
    )
    return [back4, back3, back2, back1, own]


def local(queries, keys, values, doc_ids, counts):
    device = lax.axis_index("seq")
    x = device % 4
    place = device.reshape(1)
    parts = []
    for own in pack(doc_ids, keys, values):
        parts.append(earlier_shards(own, x))
    before = None
    first = 0
    for heads, part in zip(SPLIT, parts):
        before = attend(place, counts, queries, part, first, heads, before)
        first += heads
    return before[0]


def solution(mesh):
    in_specs = (
        P(("dp", "seq"), None, None),
        P(("dp", "seq"), None, None),
        P(("dp", "seq"), None, None),
        P(("dp", "seq")),
        P("dp"),
    )
    out_specs = P(("dp", "seq"), None, None)
    return jax.shard_map(local, mesh=mesh, in_specs=in_specs, out_specs=out_specs, check_vma=False)
```

time: 53.4 us -> 44.2 us (0.83)
  waiting for transfers between devices: 14.9 us -> 10.5 us
  starting transfers between devices: 14.7 us -> 18.8 us
  other arithmetic: 3.44 us -> 0.15 us
  Pallas kernels: 16.9 us -> 13.7 us
  local copies, waits for them, and re-layouts: 3.08 us -> 0.01 us
    pallas_call x2 -> x3, Pallas kernels: 16.9 us -> 12.3 us  [attend(): pl.pallas_call(functools.partial(attend_kernel, scale=math.log2(math.e) /...]
    ppermute x6 -> x9, waiting for transfers between devices: 11.7 us -> 9.01 us  [row_permute(): lax.ppermute(array, 'seq', [(4 * r + i, 4 * r + j) for r in range(rows) f...]
    slice x6 -> x0, local copies, waits for them, and re-layouts: 2.39 us -> none  [the longest x3 1.21 us: local(): keys_by_head[first:first + heads].reshape(heads * shard, width)]
    ppermute x6 -> x9, starting transfers between devices: 7.93 us -> 10.2 us  [row_permute(): lax.ppermute(array, 'seq', [(4 * r + i, 4 * r + j) for r in range(rows) f...]
    select_n x2 -> x3, other arithmetic: 1.99 us -> 0.09 us  [earlier_shards(): jnp.where(x < 3, own, back4)]
    ppermute x2 -> x3, starting transfers between devices: 6.79 us -> 8.6 us  [earlier_shards(): back4 = lax.ppermute(own, 'seq', [(i, i + 4) for i in range(size - 4)])]
    ppermute x2 -> x3, waiting for transfers between devices: 3.2 us -> 1.51 us  [earlier_shards(): back4 = lax.ppermute(own, 'seq', [(i, i + 4) for i in range(size - 4)])]
    pallas_call x0 -> x1, Pallas kernels: none -> 1.37 us  [pack(): pl.pallas_call(pack_kernel, out_shape=[jax.ShapeDtypeStruct((r, width), j...]
  transfers between devices with their start and end apart: 8 -> 12, of which waited for: 5 -> 6; matrix products, arithmetic and copies ran while one was open for 5% -> 0% of each run, Pallas kernels for 16% -> 18%
where the time goes in v2:
time: 44.2 us; the launch traced here: 43.4 us
  starting transfers between devices  18.8 us (43%)
  Pallas kernels  13.7 us (31%)
  waiting for transfers between devices  10.5 us (24%)
    pallas_call x3, Pallas kernels, attend(): pl.pallas_call(functools.partial(attend_kernel, scale=math.log2(math.e) /...  12.3 us
    ppermute x9, starting transfers between devices, row_permute(): lax.ppermute(array, 'seq', [(4 * r + i, 4 * r + j) for r in range(rows) f...  10.2 us
    ppermute x9, waiting for transfers between devices, row_permute(): lax.ppermute(array, 'seq', [(4 * r + i, 4 * r + j) for r in range(rows) f...  9.01 us
    ppermute x3, starting transfers between devices, earlier_shards(): back4 = lax.ppermute(own, 'seq', [(i, i + 4) for i in range(size - 4)])  8.6 us
    ppermute x3, waiting for transfers between devices, earlier_shards(): back4 = lax.ppermute(own, 'seq', [(i, i + 4) for i in range(size - 4)])  1.51 us
    pallas_call x1, Pallas kernels, pack(): pl.pallas_call(pack_kernel, out_shape=[jax.ShapeDtypeStruct((r, width), j...  1.37 us
  transfers between devices with their start and end apart: 12, of which 6 were waited for; matrix products, arithmetic and copies ran while one was open for 0% of the time, Pallas kernels for 18%

profile of v2, /device:TPU:232, one launch (start us, length us, event | category | flops | bytes accessed | tf_op | source)
XLA Modules:
  0.0 43.4 jit_solution(11840487921116220868)
XLA Ops:
  0.0 0.0 copy-start
  0.0 0.0 copy-start.1
  0.0 1.4 %pack.1 = (bf16[528,128]{1,0:T(8,128)(2,1)S(1)}, bf16[768,128]{1,0:T(8,128)(2,1)S(1)}, bf16[768,128]{1,0:T(8,128)(2,1)S(1)}) custom-call(s32[1,128]{1,0:T(1,128)} %bitcast.2, bf16[128,8,128]{2,1,0:T(8,128)(2,1)} %keys_hbm.1, bf16[128,8,128]{2,1,0:T(8,128)(2,1)} %values_hbm.1), custom_call_target="tpu_custom_call" | custom-call | tf_op jit(solution)/shard_map/pack/pallas_call | solution.py:47
  1.4 3.5 %collective-permute-start.4 = (bf16[528,128]{1,0:T(8,128)(2,1)S(1)}, bf16[528,128]{1,0:T(8,128)(2,1)S(1)}, u32[]{:S(2)}, u32[]{:S(2)}) collective-permute-start(bf16[528,128]{1,0:T(8,128)(2,1)S(1)} %get-tuple-element.11.refs_4_), channel_id=1, source_target_pairs={{0,4},{1,5},{2,6},{3,7},{4,8},{5,9},{6,10},{7,11},{8,12},{9,13},{1... | collective-permute-start | bytes 405512 | tf_op jit(solution)/shard_map/ppermute | solution.py:205
  4.9 3.2 %collective-permute-start.8 = (bf16[768,128]{1,0:T(8,128)(2,1)S(1)}, bf16[768,128]{1,0:T(8,128)(2,1)S(1)}, u32[]{:S(2)}, u32[]{:S(2)}) collective-permute-start(bf16[768,128]{1,0:T(8,128)(2,1)S(1)} %get-tuple-element.13.refs_4_), channel_id=1, source_target_pairs={{0,4},{1,5},{2,6},{3,7},{4,8},{5,9},{6,10},{7,11},{8,12},{9,13},{1... | collective-permute-start | bytes 589832 | tf_op jit(solution)/shard_map/ppermute | solution.py:205
  8.1 1.9 %collective-permute-start = (bf16[768,128]{1,0:T(8,128)(2,1)S(1)}, bf16[768,128]{1,0:T(8,128)(2,1)S(1)}, u32[]{:S(2)}, u32[]{:S(2)}) collective-permute-start(bf16[768,128]{1,0:T(8,128)(2,1)S(1)} %get-tuple-element.10.refs_4_), channel_id=1, source_target_pairs={{0,4},{1,5},{2,6},{3,7},{4,8},{5,9},{6,10},{7,11},{8,12},{9,13},{1... | collective-permute-start | bytes 589832 | tf_op jit(solution)/shard_map/ppermute | solution.py:205
  10.0 0.0 collective-permute-done.4.refs_0_
  10.1 2.8 %collective-permute-start.5 = (bf16[528,128]{1,0:T(8,128)(2,1)S(1)}, bf16[528,128]{1,0:T(8,128)(2,1)S(1)}, u32[]{:S(2)}, u32[]{:S(2)}) collective-permute-start(bf16[528,128]{1,0:T(8,128)(2,1)S(1)} %get-tuple-element.20), channel_id=1, source_target_pairs={{0,3},{1,0},{2,1},{3,2},{4,7},{5,4},{6,5},{7,6},{8,11},{9,8},{10,9... | collective-permute-start | bytes 405512 | tf_op jit(solution)/shard_map/ppermute | solution.py:200
  12.9 0.0 collective-permute-start.6
  12.9 1.5 %collective-permute-done.8.refs_0_ = bf16[768,128]{1,0:T(8,128)(2,1)S(1)} collective-permute-done((bf16[768,128]{1,0:T(8,128)(2,1)S(1)}, bf16[768,128]{1,0:T(8,128)(2,1)S(1)}, u32[]{:S(2)}, u32[]{:S(2)}) %collective-permute-start.8) | collective-permute-done | bytes 196640 | tf_op jit(solution)/shard_map/ppermute | solution.py:205
  14.5 1.6 %collective-permute-start.10 = (bf16[768,128]{1,0:T(8,128)(2,1)S(1)}, bf16[768,128]{1,0:T(8,128)(2,1)S(1)}, u32[]{:S(2)}, u32[]{:S(2)}) collective-permute-start(bf16[768,128]{1,0:T(8,128)(2,1)S(1)} %get-tuple-element.15), channel_id=1, source_target_pairs={{0,1},{1,2},{2,3},{3,0},{4,5},{5,6},{6,7},{7,4},{8,9},{9,10},{10,1... | collective-permute-start | bytes 589832 | tf_op jit(solution)/shard_map/ppermute | solution.py:200
  16.0 1.7 %collective-permute-start.9 = (bf16[768,128]{1,0:T(8,128)(2,1)S(1)}, bf16[768,128]{1,0:T(8,128)(2,1)S(1)}, u32[]{:S(2)}, u32[]{:S(2)}) collective-permute-start(bf16[768,128]{1,0:T(8,128)(2,1)S(1)} %get-tuple-element.16), channel_id=1, source_target_pairs={{0,3},{1,0},{2,1},{3,2},{4,7},{5,4},{6,5},{7,6},{8,11},{9,8},{10,9... | collective-permute-start | bytes 589832 | tf_op jit(solution)/shard_map/ppermute | solution.py:200
  17.8 0.0 collective-permute-done.refs_0_
  17.8 2.4 %collective-permute-start.1 = (bf16[768,128]{1,0:T(8,128)(2,1)S(1)}, bf16[768,128]{1,0:T(8,128)(2,1)S(1)}, u32[]{:S(2)}, u32[]{:S(2)}) collective-permute-start(bf16[768,128]{1,0:T(8,128)(2,1)S(1)} %get-tuple-element.18), channel_id=1, source_target_pairs={{0,3},{1,0},{2,1},{3,2},{4,7},{5,4},{6,5},{7,6},{8,11},{9,8},{10,9... | collective-permute-start | bytes 589832 | tf_op jit(solution)/shard_map/ppermute | solution.py:200
  20.2 0.0 collective-permute-done.5.refs_1_
  20.2 0.0 collective-permute-start.2
  20.2 0.4 collective-permute-done.6.refs_3_
  20.6 0.5 %collective-permute-start.7 = (bf16[528,128]{1,0:T(8,128)(2,1)S(1)}, bf16[528,128]{1,0:T(8,128)(2,1)S(1)}, u32[]{:S(2)}, u32[]{:S(2)}) collective-permute-start(bf16[528,128]{1,0:T(8,128)(2,1)S(1)} %broadcast_select_fusion.7), channel_id=1, source_target_pairs={{0,1},{1,0},{2,3},{3,2},{4,5},{5,4},{6,7},{7,6},{8,9},{9,8},{10,11... | collective-permute-start | bytes 405512 | tf_op jit(solution)/shard_map/ppermute | solution.py:200
  21.1 2.0 %collective-permute-done.10.refs_3_ = bf16[768,128]{1,0:T(8,128)(2,1)S(1)} collective-permute-done((bf16[768,128]{1,0:T(8,128)(2,1)S(1)}, bf16[768,128]{1,0:T(8,128)(2,1)S(1)}, u32[]{:S(2)}, u32[]{:S(2)}) %collective-permute-start.10) | collective-permute-done | bytes 196640 | tf_op jit(solution)/shard_map/ppermute | solution.py:200
  23.1 0.7 %collective-permute-done.9.refs_1_ = bf16[768,128]{1,0:T(8,128)(2,1)S(1)} collective-permute-done((bf16[768,128]{1,0:T(8,128)(2,1)S(1)}, bf16[768,128]{1,0:T(8,128)(2,1)S(1)}, u32[]{:S(2)}, u32[]{:S(2)}) %collective-permute-start.9) | collective-permute-done | bytes 196640 | tf_op jit(solution)/shard_map/ppermute | solution.py:200
  23.8 0.9 %collective-permute-start.11 = (bf16[768,128]{1,0:T(8,128)(2,1)S(1)}, bf16[768,128]{1,0:T(8,128)(2,1)S(1)}, u32[]{:S(2)}, u32[]{:S(2)}) collective-permute-start(bf16[768,128]{1,0:T(8,128)(2,1)S(1)} %broadcast_select_fusion.2), channel_id=1, source_target_pairs={{0,1},{1,0},{2,3},{3,2},{4,5},{5,4},{6,7},{7,6},{8,9},{9,8},{10,11... | collective-permute-start | bytes 589832 | tf_op jit(solution)/shard_map/ppermute | solution.py:200
  24.7 3.3 %collective-permute-done.1.refs_1_ = bf16[768,128]{1,0:T(8,128)(2,1)S(1)} collective-permute-done((bf16[768,128]{1,0:T(8,128)(2,1)S(1)}, bf16[768,128]{1,0:T(8,128)(2,1)S(1)}, u32[]{:S(2)}, u32[]{:S(2)}) %collective-permute-start.1) | collective-permute-done | bytes 196640 | tf_op jit(solution)/shard_map/ppermute | solution.py:200
  28.0 0.0 collective-permute-done.2.refs_3_
  28.0 0.3 collective-permute-start.3
  28.3 2.6 %collective-permute-done.7.refs_2_ = bf16[528,128]{1,0:T(8,128)(2,1)S(1)} collective-permute-done((bf16[528,128]{1,0:T(8,128)(2,1)S(1)}, bf16[528,128]{1,0:T(8,128)(2,1)S(1)}, u32[]{:S(2)}, u32[]{:S(2)}) %collective-permute-start.7) | collective-permute-done | bytes 135200 | tf_op jit(solution)/shard_map/ppermute | solution.py:200
  30.9 0.0 copy-done
  30.9 0.0 copy-done.1
  30.9 3.5 %attend.3 = (bf16[128,64,128]{2,1,0:T(8,128)(2,1)}, bf16[640,128]{1,0:T(8,128)(2,1)S(1)}) custom-call(s32[1]{0:T(128)} %bitcast.place, s32[16]{0:T(128)S(1)} %copy-done.1, bf16[128,64,128]{2,1,0:T(8,128)(2,1)S(1)} %copy-done, bf16[528,128]{1,0:T(8,128)(2,1)S(1)} %collective-permute-done.4.refs_0_, bf16[528,128]{1,0:T(8,128)(2,1)S(1)} %collective-permute-done.5.refs_1_, ...), custom_call_target="tpu_custom_call" | custom-call | flops 671088640 | bytes 1703936 | tf_op jit(solution)/shard_map/attend/pallas_call | solution.py:168
  34.4 0.0 collective-permute-done.11.refs_2_
  34.4 4.4 %attend.4.refs_6_ = bf16[128,64,128]{2,1,0:T(8,128)(2,1)} custom-call(s32[1]{0:T(128)} %bitcast.place, s32[16]{0:T(128)S(1)} %copy-done.1, bf16[128,64,128]{2,1,0:T(8,128)(2,1)S(1)} %copy-done, bf16[768,128]{1,0:T(8,128)(2,1)S(1)} %collective-permute-done.8.refs_0_, ...), custom_call_target="tpu_custom_call", output_to_operand_aliasing={{}: (9, {})} | custom-call | flops 1006632960 | bytes 2555904 | tf_op jit(solution)/shard_map/attend/pallas_call | solution.py:168
  38.8 0.0 collective-permute-done.3.refs_2_
  38.8 4.4 %attend.5 = bf16[128,64,128]{2,1,0:T(8,128)(2,1)} custom-call(s32[1]{0:T(128)} %bitcast.place, s32[16]{0:T(128)S(1)} %copy-done.1, bf16[128,64,128]{2,1,0:T(8,128)(2,1)S(1)} %copy-done, bf16[768,128]{1,0:T(8,128)(2,1)S(1)} %collective-permute-done.refs_0_, bf16[768,128]{1,0:T(8,128)(2,1)S(1)} %collective-permute-done.1.refs_1_, ...), custom_call_target="tpu_custom_call", output_to_operand_aliasing={{}: (9, {})} | custom-call | flops 1006632960 | bytes 2555904 | tf_op jit(solution)/shard_map/attend/pallas_call | solution.py:168
  (6 shorter events, 0.2 us)
Async XLA Ops:
  0.0 30.9 %copy-start = (bf16[128,64,128]{2,1,0:T(8,128)(2,1)S(1)}, bf16[128,64,128]{2,1,0:T(8,128)(2,1)}, u32[]{:S(2)}) copy-start(bf16[128,64,128]{2,1,0:T(8,128)(2,1)} %q_ref.5) | copy-start | bytes 6291460
  0.0 30.9 %copy-start.1 = (s32[16]{0:T(128)S(1)}, s32[16]{0:T(128)}, u32[]{:S(2)}) copy-start(s32[16]{0:T(128)} %counts.5) | copy-start | bytes 196
  1.4 8.7 %collective-permute-start.4 = (bf16[528,128]{1,0:T(8,128)(2,1)S(1)}, bf16[528,128]{1,0:T(8,128)(2,1)S(1)}, u32[]{:S(2)}, u32[]{:S(2)}) collective-permute-start(bf16[528,128]{1,0:T(8,128)(2,1)S(1)} %get-tuple-element.11.refs_4_), channel_id=1, source_target_pairs={{0,4},{1,5},{2,6},{3,7},{4,8},{5,9},{6,10},{7,11},{8,12},{9,13},{1... | collective-permute-start | bytes 405512 | tf_op jit(solution)/shard_map/ppermute | solution.py:205
  4.9 9.5 %collective-permute-start.8 = (bf16[768,128]{1,0:T(8,128)(2,1)S(1)}, bf16[768,128]{1,0:T(8,128)(2,1)S(1)}, u32[]{:S(2)}, u32[]{:S(2)}) collective-permute-start(bf16[768,128]{1,0:T(8,128)(2,1)S(1)} %get-tuple-element.13.refs_4_), channel_id=1, source_target_pairs={{0,4},{1,5},{2,6},{3,7},{4,8},{5,9},{6,10},{7,11},{8,12},{9,13},{1... | collective-permute-start | bytes 589832 | tf_op jit(solution)/shard_map/ppermute | solution.py:205
  8.1 9.7 %collective-permute-start = (bf16[768,128]{1,0:T(8,128)(2,1)S(1)}, bf16[768,128]{1,0:T(8,128)(2,1)S(1)}, u32[]{:S(2)}, u32[]{:S(2)}) collective-permute-start(bf16[768,128]{1,0:T(8,128)(2,1)S(1)} %get-tuple-element.10.refs_4_), channel_id=1, source_target_pairs={{0,4},{1,5},{2,6},{3,7},{4,8},{5,9},{6,10},{7,11},{8,12},{9,13},{1... | collective-permute-start | bytes 589832 | tf_op jit(solution)/shard_map/ppermute | solution.py:205
  10.1 10.1 %collective-permute-start.5 = (bf16[528,128]{1,0:T(8,128)(2,1)S(1)}, bf16[528,128]{1,0:T(8,128)(2,1)S(1)}, u32[]{:S(2)}, u32[]{:S(2)}) collective-permute-start(bf16[528,128]{1,0:T(8,128)(2,1)S(1)} %get-tuple-element.20), channel_id=1, source_target_pairs={{0,3},{1,0},{2,1},{3,2},{4,7},{5,4},{6,5},{7,6},{8,11},{9,8},{10,9... | collective-permute-start | bytes 405512 | tf_op jit(solution)/shard_map/ppermute | solution.py:200
  12.9 7.7 %collective-permute-start.6 = (bf16[528,128]{1,0:T(8,128)(2,1)S(1)}, bf16[528,128]{1,0:T(8,128)(2,1)S(1)}, u32[]{:S(2)}, u32[]{:S(2)}) collective-permute-start(bf16[528,128]{1,0:T(8,128)(2,1)S(1)} %get-tuple-element.19), channel_id=1, source_target_pairs={{0,1},{1,2},{2,3},{3,0},{4,5},{5,6},{6,7},{7,4},{8,9},{9,10},{10,1... | collective-permute-start | bytes 405512 | tf_op jit(solution)/shard_map/ppermute | solution.py:200
  14.5 8.6 %collective-permute-start.10 = (bf16[768,128]{1,0:T(8,128)(2,1)S(1)}, bf16[768,128]{1,0:T(8,128)(2,1)S(1)}, u32[]{:S(2)}, u32[]{:S(2)}) collective-permute-start(bf16[768,128]{1,0:T(8,128)(2,1)S(1)} %get-tuple-element.15), channel_id=1, source_target_pairs={{0,1},{1,2},{2,3},{3,0},{4,5},{5,6},{6,7},{7,4},{8,9},{9,10},{10,1... | collective-permute-start | bytes 589832 | tf_op jit(solution)/shard_map/ppermute | solution.py:200
  16.0 7.8 %collective-permute-start.9 = (bf16[768,128]{1,0:T(8,128)(2,1)S(1)}, bf16[768,128]{1,0:T(8,128)(2,1)S(1)}, u32[]{:S(2)}, u32[]{:S(2)}) collective-permute-start(bf16[768,128]{1,0:T(8,128)(2,1)S(1)} %get-tuple-element.16), channel_id=1, source_target_pairs={{0,3},{1,0},{2,1},{3,2},{4,7},{5,4},{6,5},{7,6},{8,11},{9,8},{10,9... | collective-permute-start | bytes 589832 | tf_op jit(solution)/shard_map/ppermute | solution.py:200
  17.8 10.2 %collective-permute-start.1 = (bf16[768,128]{1,0:T(8,128)(2,1)S(1)}, bf16[768,128]{1,0:T(8,128)(2,1)S(1)}, u32[]{:S(2)}, u32[]{:S(2)}) collective-permute-start(bf16[768,128]{1,0:T(8,128)(2,1)S(1)} %get-tuple-element.18), channel_id=1, source_target_pairs={{0,3},{1,0},{2,1},{3,2},{4,7},{5,4},{6,5},{7,6},{8,11},{9,8},{10,9... | collective-permute-start | bytes 589832 | tf_op jit(solution)/shard_map/ppermute | solution.py:200
  20.2 7.8 %collective-permute-start.2 = (bf16[768,128]{1,0:T(8,128)(2,1)S(1)}, bf16[768,128]{1,0:T(8,128)(2,1)S(1)}, u32[]{:S(2)}, u32[]{:S(2)}) collective-permute-start(bf16[768,128]{1,0:T(8,128)(2,1)S(1)} %get-tuple-element.17), channel_id=1, source_target_pairs={{0,1},{1,2},{2,3},{3,0},{4,5},{5,6},{6,7},{7,4},{8,9},{9,10},{10,1... | collective-permute-start | bytes 589832 | tf_op jit(solution)/shard_map/ppermute | solution.py:200
  20.6 10.3 %collective-permute-start.7 = (bf16[528,128]{1,0:T(8,128)(2,1)S(1)}, bf16[528,128]{1,0:T(8,128)(2,1)S(1)}, u32[]{:S(2)}, u32[]{:S(2)}) collective-permute-start(bf16[528,128]{1,0:T(8,128)(2,1)S(1)} %broadcast_select_fusion.7), channel_id=1, source_target_pairs={{0,1},{1,0},{2,3},{3,2},{4,5},{5,4},{6,7},{7,6},{8,9},{9,8},{10,11... | collective-permute-start | bytes 405512 | tf_op jit(solution)/shard_map/ppermute | solution.py:200
  23.8 10.6 %collective-permute-start.11 = (bf16[768,128]{1,0:T(8,128)(2,1)S(1)}, bf16[768,128]{1,0:T(8,128)(2,1)S(1)}, u32[]{:S(2)}, u32[]{:S(2)}) collective-permute-start(bf16[768,128]{1,0:T(8,128)(2,1)S(1)} %broadcast_select_fusion.2), channel_id=1, source_target_pairs={{0,1},{1,0},{2,3},{3,2},{4,5},{5,4},{6,7},{7,6},{8,9},{9,8},{10,11... | collective-permute-start | bytes 589832 | tf_op jit(solution)/shard_map/ppermute | solution.py:200
  28.0 10.8 %collective-permute-start.3 = (bf16[768,128]{1,0:T(8,128)(2,1)S(1)}, bf16[768,128]{1,0:T(8,128)(2,1)S(1)}, u32[]{:S(2)}, u32[]{:S(2)}) collective-permute-start(bf16[768,128]{1,0:T(8,128)(2,1)S(1)} %broadcast_select_fusion.3), channel_id=1, source_target_pairs={{0,1},{1,0},{2,3},{3,2},{4,5},{5,4},{6,7},{7,6},{8,9},{9,8},{10,11... | collective-permute-start | bytes 589832 | tf_op jit(solution)/shard_map/ppermute | solution.py:200

commit v3 on v2

--- a/solution.py
+++ b/solution.py
@@ -79,18 +79,36 @@
         mask[i * shard : (i + 1) * shard, :] = jnp.where(allowed, 0.0, MASKED).astype(jnp.bfloat16)
 
 
-def attend_kernel(place, counts, q_ref, *refs, scale, first, heads, makes_mask):
+def attend_kernel(place, counts, q_ref, *refs, scale, starts, heads, makes_mask):
     blocks = len(BACK)
-    parts, refs = refs[:blocks], refs[blocks:]
+    parts, refs = refs[:blocks], list(refs[blocks:])
     shard, _, width = q_ref.shape
     group = GROUP
+    first = starts[-1]
+    last = first + heads == sum(SPLIT)
+    mask = refs.pop(0) if not makes_mask else None
+    others = [refs.pop(0) for _ in starts[:-1]] if last else []
+    out_ref = refs.pop(0)
     if makes_mask:
-        result, mask, *refs = refs
+        mask = refs.pop(0)
         at = 2 * heads * shard
         fill_mask(place, counts, [p[at : at + 1, :] for p in parts], mask, shard)
-    else:
-        mask, _, result, *refs = refs
-    select, key_window, value_window, mixed_heads, sent = refs
+    select, key_window, value_window = refs[:3]
+    copies = []
+
+    def send(source, rows, head):
+        at = head * group
+        copies.append(
+            pltpu.make_async_copy(
+                source, out_ref.at[rows, at : at + group, :], refs[4].at[len(copies)]
+            )
+        )
+        copies[-1].start()
+
+    for other, start in zip(others, starts):
+        for j in range(other.shape[0]):
+            send(other.at[j], slice(0, shard), start + j)
+    mixed_heads = refs[3] if last else out_ref
     position = lax.broadcasted_iota(jnp.int32, (shard * group, shard), 0) // group
     column = lax.broadcasted_iota(jnp.int32, (shard * group, shard), 1)
     select[...] = jnp.where(position == column, 1.0, 0.0).astype(jnp.bfloat16)
@@ -116,12 +134,6 @@
         weights = jnp.exp2((scores - top) * scale)
         return weights.astype(jnp.bfloat16), jnp.sum(weights, axis=1, keepdims=True)
 
-    def leave(j):
-        at = (first + j) * group
-        return pltpu.make_async_copy(
-            mixed_heads.at[j], result.at[:, at : at + group, :], sent.at[j]
-        )
-
     def mix(j, c, weights, norm):
         mixed = jnp.dot(weights, value_window[j], preferred_element_type=jnp.float32)
         position = lax.broadcasted_iota(jnp.int32, (ROWS, 1), 0) // group + c * tall
@@ -129,8 +141,9 @@
         mixed_heads[j, c * tall : (c + 1) * tall] = (
             (mixed * inverse).astype(jnp.bfloat16).reshape(tall, group, width)
         )
-        if (c + 1) * tall == shard:
-            leave(j).start()
+        if last:
+            rows = slice(c * tall, (c + 1) * tall)
+            send(mixed_heads.at[j, rows], rows, first + j)
 
     work = [(j, c) for j in range(heads) for c in range(shard // tall)]
     scores = score(*work[0])
@@ -143,47 +156,53 @@
         waiting = (j, c, weights, norm)
         scores = after
     mix(*waiting)
-    for j in range(heads):
-        leave(j).wait()
-
-
-def attend(place, counts, queries, parts, first, heads, before):
+    for copy in copies:
+        copy.wait()
+
+
+def attend(place, counts, queries, parts, starts, heads, mask, others):
     shard, _, width = queries.shape
     window = len(BACK) * shard
+    last = starts[-1] + heads == sum(SPLIT)
     vmem = pl.BlockSpec(memory_space=pltpu.VMEM)
     in_specs = [pl.BlockSpec(memory_space=pltpu.SMEM)] * 2 + [vmem] * (1 + len(BACK))
     operands = [place, counts, queries, *parts]
-    out_shape = [jax.ShapeDtypeStruct(queries.shape, jnp.bfloat16)]
-    out_specs = [pl.BlockSpec(memory_space=pltpu.HBM)]
-    aliases = {}
-    if before is None:
+    mixed = (heads, shard, GROUP, width)
+    if last:
+        out_shape = [jax.ShapeDtypeStruct(queries.shape, jnp.bfloat16)]
+        out_specs = [pl.BlockSpec(memory_space=pltpu.HBM)]
+    else:
+        out_shape = [jax.ShapeDtypeStruct(mixed, jnp.bfloat16)]
+        out_specs = [vmem]
+    if mask is None:
         out_shape.append(jax.ShapeDtypeStruct((window, shard), jnp.bfloat16))
         out_specs.append(vmem)
     else:
-        result, mask = before
-        in_specs += [vmem, pl.BlockSpec(memory_space=pltpu.HBM)]
-        aliases = {len(operands) + 1: 0}
-        operands += [mask, result]
+        operands.append(mask)
+        in_specs.append(vmem)
+    scratch = [
+        pltpu.VMEM((shard * GROUP, shard), jnp.bfloat16),
+        pltpu.VMEM((heads, window, 2 * width), jnp.bfloat16),
+        pltpu.VMEM((heads, window, width), jnp.bfloat16),
+    ]
+    if last:
+        operands += others
+        in_specs += [vmem] * len(others)
+        pieces = starts[-1] + heads * (shard * GROUP // ROWS)
+        scratch += [pltpu.VMEM(mixed, jnp.bfloat16), pltpu.SemaphoreType.DMA((pieces,))]
     rows = shard * GROUP * heads
     out = pl.pallas_call(
         functools.partial(
             attend_kernel,
             scale=math.log2(math.e) / math.sqrt(width),
-            first=first,
+            starts=tuple(starts),
             heads=heads,
-            makes_mask=before is None,
+            makes_mask=mask is None,
         ),
         out_shape=out_shape,
         in_specs=in_specs,
         out_specs=out_specs,
-        scratch_shapes=[
-            pltpu.VMEM((shard * GROUP, shard), jnp.bfloat16),
-            pltpu.VMEM((heads, window, 2 * width), jnp.bfloat16),
-            pltpu.VMEM((heads, window, width), jnp.bfloat16),
-            pltpu.VMEM((heads, shard, GROUP, width), jnp.bfloat16),
-            pltpu.SemaphoreType.DMA((heads,)),
-        ],
-        input_output_aliases=aliases,
+        scratch_shapes=scratch,
         compiler_params=pltpu.CompilerParams(vmem_limit_bytes=32 << 20),
         cost_estimate=pl.CostEstimate(
             flops=4 * rows * window * width,
@@ -192,7 +211,7 @@
         ),
         name="attend",
     )(*operands)
-    return out if before is None else [out[0], mask]
+    return out[0], out[1] if mask is None else mask
 
 
 def row_permute(array, pairs):
@@ -200,11 +219,17 @@
     return lax.ppermute(array, "seq", [(4 * r + i, 4 * r + j) for r in range(rows) for i, j in pairs])
 
 
-def earlier_shards(own, x):
+def earlier_shards(own, x, direct):
     size = lax.axis_size("seq")
-    back4 = lax.ppermute(own, "seq", [(i, i + 4) for i in range(size - 4)])
-    back1 = row_permute(jnp.where(x < 3, own, back4), [(0, 1), (1, 2), (2, 3), (3, 0)])
-    back3 = row_permute(jnp.where(x < 1, own, back4), [(0, 3), (1, 0), (2, 1), (3, 2)])
+    back4 = lax.ppermute(own, "seq", [(i, (i + 4) % size) for i in range(size)])
+    if direct:
+        back3 = lax.ppermute(own, "seq", [(i, (i + 3) % size) for i in range(size)])
+    else:
+        back3 = row_permute(jnp.where(x < 1, own, back4), [(0, 3), (1, 0), (2, 1), (3, 2)])
+    if direct:
+        back1 = lax.ppermute(own, "seq", [(i, (i + 1) % size) for i in range(size)])
+    else:
+        back1 = row_permute(jnp.where(x < 3, own, back4), [(0, 1), (1, 2), (2, 3), (3, 0)])
     back2 = row_permute(
         jnp.where(x % 2 == 0, back1, back3), [(0, 1), (1, 0), (2, 3), (3, 2)]
     )
@@ -217,13 +242,14 @@
     place = device.reshape(1)
     parts = []
     for own in pack(doc_ids, keys, values):
-        parts.append(earlier_shards(own, x))
-    before = None
-    first = 0
-    for heads, part in zip(SPLIT, parts):
-        before = attend(place, counts, queries, part, first, heads, before)
-        first += heads
-    return before[0]
+        parts.append(earlier_shards(own, x, False))
+    mask = None
+    starts, mixed = [], []
+    for i, (heads, part) in enumerate(zip(SPLIT, parts)):
+        starts.append(sum(SPLIT[:i]))
+        out, mask = attend(place, counts, queries, part, starts, heads, mask, mixed)
+        mixed.append(out)
+    return mixed[-1]
 
 
 def solution(mesh):

time: 44.2 us -> 45.5 us (1.029)
  the two profiles are of different devices: /device:TPU:232 before, /device:TPU:64 now
where the time goes in v3:
time: 45.5 us
  waiting for transfers between devices  16.4 us (36%)
  starting transfers between devices  16.3 us (36%)
  Pallas kernels  12.3 us (27%)
    ppermute x9, starting transfers between devices, row_permute(): lax.ppermute(array, 'seq', [(4 * r + i, 4 * r + j) for r in range(rows) f...  11.8 us
    pallas_call x3, Pallas kernels, attend(): pl.pallas_call(functools.partial(attend_kernel, scale=math.log2(math.e) /...  11 us
    ppermute x9, waiting for transfers between devices, row_permute(): lax.ppermute(array, 'seq', [(4 * r + i, 4 * r + j) for r in range(rows) f...  9.17 us
    ppermute x3, waiting for transfers between devices, earlier_shards(): back4 = lax.ppermute(own, 'seq', [(i, (i + 4) % size) for i in range(size)])  7.25 us
    ppermute x3, starting transfers between devices, earlier_shards(): back4 = lax.ppermute(own, 'seq', [(i, (i + 4) % size) for i in range(size)])  4.51 us
    pallas_call x1, Pallas kernels, pack(): pl.pallas_call(pack_kernel, out_shape=[jax.ShapeDtypeStruct((r, width), j...  1.37 us
  transfers between devices with their start and end apart: 12, of which 8 were waited for; matrix products, arithmetic and copies ran while one was open for 0% of the time, Pallas kernels for 14%

profile of v3, /device:TPU:64, one launch (start us, length us, event | category | flops | bytes accessed | tf_op | source)
XLA Modules:
  0.0 45.5 jit_solution(7780596285346993251)
XLA Ops:
  0.0 0.0 copy-start
  0.0 0.0 copy-start.1
  0.0 1.4 %pack.1 = (bf16[528,128]{1,0:T(8,128)(2,1)S(1)}, bf16[768,128]{1,0:T(8,128)(2,1)S(1)}, bf16[768,128]{1,0:T(8,128)(2,1)S(1)}) custom-call(s32[1,128]{1,0:T(1,128)} %bitcast.2, bf16[128,8,128]{2,1,0:T(8,128)(2,1)} %keys_hbm.1, bf16[128,8,128]{2,1,0:T(8,128)(2,1)} %values_hbm.1), custom_call_target="tpu_custom_call" | custom-call | tf_op jit(solution)/shard_map/pack/pallas_call | solution.py:47
  1.4 1.7 %collective-permute-start.4 = (bf16[528,128]{1,0:T(8,128)(2,1)S(1)}, bf16[528,128]{1,0:T(8,128)(2,1)S(1)}, u32[]{:S(2)}, u32[]{:S(2)}) collective-permute-start(bf16[528,128]{1,0:T(8,128)(2,1)S(1)} %get-tuple-element.11.refs_4_), channel_id=1, source_target_pairs={{0,4},{1,5},{2,6},{3,7},{4,8},{5,9},{6,10},{7,11},{8,12},{9,13},{1... | collective-permute-start | bytes 405512 | tf_op jit(solution)/shard_map/ppermute | solution.py:224
  3.0 1.6 %collective-permute-start = (bf16[768,128]{1,0:T(8,128)(2,1)S(1)}, bf16[768,128]{1,0:T(8,128)(2,1)S(1)}, u32[]{:S(2)}, u32[]{:S(2)}) collective-permute-start(bf16[768,128]{1,0:T(8,128)(2,1)S(1)} %get-tuple-element.10.refs_4_), channel_id=1, source_target_pairs={{0,4},{1,5},{2,6},{3,7},{4,8},{5,9},{6,10},{7,11},{8,12},{9,13},{1... | collective-permute-start | bytes 589832 | tf_op jit(solution)/shard_map/ppermute | solution.py:224
  4.6 1.3 %collective-permute-start.8 = (bf16[768,128]{1,0:T(8,128)(2,1)S(1)}, bf16[768,128]{1,0:T(8,128)(2,1)S(1)}, u32[]{:S(2)}, u32[]{:S(2)}) collective-permute-start(bf16[768,128]{1,0:T(8,128)(2,1)S(1)} %get-tuple-element.14.refs_4_), channel_id=1, source_target_pairs={{0,4},{1,5},{2,6},{3,7},{4,8},{5,9},{6,10},{7,11},{8,12},{9,13},{1... | collective-permute-start | bytes 589832 | tf_op jit(solution)/shard_map/ppermute | solution.py:224
  5.9 3.2 %collective-permute-done.4.refs_0_ = bf16[528,128]{1,0:T(8,128)(2,1)S(1)} collective-permute-done((bf16[528,128]{1,0:T(8,128)(2,1)S(1)}, bf16[528,128]{1,0:T(8,128)(2,1)S(1)}, u32[]{:S(2)}, u32[]{:S(2)}) %collective-permute-start.4) | collective-permute-done | bytes 135200 | tf_op jit(solution)/shard_map/ppermute | solution.py:224
  9.2 1.6 %collective-permute-start.6 = (bf16[528,128]{1,0:T(8,128)(2,1)S(1)}, bf16[528,128]{1,0:T(8,128)(2,1)S(1)}, u32[]{:S(2)}, u32[]{:S(2)}) collective-permute-start(bf16[528,128]{1,0:T(8,128)(2,1)S(1)} %get-tuple-element.19), channel_id=1, source_target_pairs={{0,1},{1,2},{2,3},{3,0},{4,5},{5,6},{6,7},{7,4},{8,9},{9,10},{10,1... | collective-permute-start | bytes 405512 | tf_op jit(solution)/shard_map/ppermute | solution.py:219
  10.7 1.7 %collective-permute-start.5 = (bf16[528,128]{1,0:T(8,128)(2,1)S(1)}, bf16[528,128]{1,0:T(8,128)(2,1)S(1)}, u32[]{:S(2)}, u32[]{:S(2)}) collective-permute-start(bf16[528,128]{1,0:T(8,128)(2,1)S(1)} %get-tuple-element.20), channel_id=1, source_target_pairs={{0,3},{1,0},{2,1},{3,2},{4,7},{5,4},{6,5},{7,6},{8,11},{9,8},{10,9... | collective-permute-start | bytes 405512 | tf_op jit(solution)/shard_map/ppermute | solution.py:219
  12.5 4.0 %collective-permute-done.8.refs_0_ = bf16[768,128]{1,0:T(8,128)(2,1)S(1)} collective-permute-done((bf16[768,128]{1,0:T(8,128)(2,1)S(1)}, bf16[768,128]{1,0:T(8,128)(2,1)S(1)}, u32[]{:S(2)}, u32[]{:S(2)}) %collective-permute-start.8) | collective-permute-done | bytes 196640 | tf_op jit(solution)/shard_map/ppermute | solution.py:224
  16.5 1.6 %collective-permute-start.10 = (bf16[768,128]{1,0:T(8,128)(2,1)S(1)}, bf16[768,128]{1,0:T(8,128)(2,1)S(1)}, u32[]{:S(2)}, u32[]{:S(2)}) collective-permute-start(bf16[768,128]{1,0:T(8,128)(2,1)S(1)} %get-tuple-element.15), channel_id=1, source_target_pairs={{0,1},{1,2},{2,3},{3,0},{4,5},{5,6},{6,7},{7,4},{8,9},{9,10},{10,1... | collective-permute-start | bytes 589832 | tf_op jit(solution)/shard_map/ppermute | solution.py:219
  18.1 1.7 %collective-permute-start.9 = (bf16[768,128]{1,0:T(8,128)(2,1)S(1)}, bf16[768,128]{1,0:T(8,128)(2,1)S(1)}, u32[]{:S(2)}, u32[]{:S(2)}) collective-permute-start(bf16[768,128]{1,0:T(8,128)(2,1)S(1)} %get-tuple-element.16), channel_id=1, source_target_pairs={{0,3},{1,0},{2,1},{3,2},{4,7},{5,4},{6,5},{7,6},{8,11},{9,8},{10,9... | collective-permute-start | bytes 589832 | tf_op jit(solution)/shard_map/ppermute | solution.py:219
  19.8 0.0 collective-permute-done.refs_0_
  19.9 0.4 collective-permute-start.2
  20.2 0.0 collective-permute-done.6.refs_3_
  20.2 3.0 %collective-permute-start.1 = (bf16[768,128]{1,0:T(8,128)(2,1)S(1)}, bf16[768,128]{1,0:T(8,128)(2,1)S(1)}, u32[]{:S(2)}, u32[]{:S(2)}) collective-permute-start(bf16[768,128]{1,0:T(8,128)(2,1)S(1)} %get-tuple-element.18), channel_id=1, source_target_pairs={{0,3},{1,0},{2,1},{3,2},{4,7},{5,4},{6,5},{7,6},{8,11},{9,8},{10,9... | collective-permute-start | bytes 589832 | tf_op jit(solution)/shard_map/ppermute | solution.py:219
  23.2 0.0 collective-permute-done.5.refs_1_
  23.2 0.1 collective-permute-start.7
  23.3 1.8 %collective-permute-done.10.refs_3_ = bf16[768,128]{1,0:T(8,128)(2,1)S(1)} collective-permute-done((bf16[768,128]{1,0:T(8,128)(2,1)S(1)}, bf16[768,128]{1,0:T(8,128)(2,1)S(1)}, u32[]{:S(2)}, u32[]{:S(2)}) %collective-permute-start.10) | collective-permute-done | bytes 196640 | tf_op jit(solution)/shard_map/ppermute | solution.py:219
  25.1 0.8 %collective-permute-done.9.refs_1_ = bf16[768,128]{1,0:T(8,128)(2,1)S(1)} collective-permute-done((bf16[768,128]{1,0:T(8,128)(2,1)S(1)}, bf16[768,128]{1,0:T(8,128)(2,1)S(1)}, u32[]{:S(2)}, u32[]{:S(2)}) %collective-permute-start.9) | collective-permute-done | bytes 196640 | tf_op jit(solution)/shard_map/ppermute | solution.py:219
  25.9 1.5 %collective-permute-start.11 = (bf16[768,128]{1,0:T(8,128)(2,1)S(1)}, bf16[768,128]{1,0:T(8,128)(2,1)S(1)}, u32[]{:S(2)}, u32[]{:S(2)}) collective-permute-start(bf16[768,128]{1,0:T(8,128)(2,1)S(1)} %broadcast_select_fusion.2), channel_id=1, source_target_pairs={{0,1},{1,0},{2,3},{3,2},{4,5},{5,4},{6,7},{7,6},{8,9},{9,8},{10,11... | collective-permute-start | bytes 589832 | tf_op jit(solution)/shard_map/ppermute | solution.py:219
  27.4 0.5 %collective-permute-done.2.refs_3_ = bf16[768,128]{1,0:T(8,128)(2,1)S(1)} collective-permute-done((bf16[768,128]{1,0:T(8,128)(2,1)S(1)}, bf16[768,128]{1,0:T(8,128)(2,1)S(1)}, u32[]{:S(2)}, u32[]{:S(2)}) %collective-permute-start.2) | collective-permute-done | bytes 196640 | tf_op jit(solution)/shard_map/ppermute | solution.py:219
  27.9 2.2 %collective-permute-done.1.refs_1_ = bf16[768,128]{1,0:T(8,128)(2,1)S(1)} collective-permute-done((bf16[768,128]{1,0:T(8,128)(2,1)S(1)}, bf16[768,128]{1,0:T(8,128)(2,1)S(1)}, u32[]{:S(2)}, u32[]{:S(2)}) %collective-permute-start.1) | collective-permute-done | bytes 196640 | tf_op jit(solution)/shard_map/ppermute | solution.py:219
  30.1 0.3 collective-permute-start.3
  30.4 2.6 %collective-permute-done.7.refs_2_ = bf16[528,128]{1,0:T(8,128)(2,1)S(1)} collective-permute-done((bf16[528,128]{1,0:T(8,128)(2,1)S(1)}, bf16[528,128]{1,0:T(8,128)(2,1)S(1)}, u32[]{:S(2)}, u32[]{:S(2)}) %collective-permute-start.7) | collective-permute-done | bytes 135200 | tf_op jit(solution)/shard_map/ppermute | solution.py:219
  33.0 0.0 copy-done
  33.0 0.0 copy-done.1
  33.0 2.8 %attend.3 = (bf16[2,128,8,128]{3,2,1,0:T(8,128)(2,1)S(1)}, bf16[640,128]{1,0:T(8,128)(2,1)S(1)}) custom-call(s32[1]{0:T(128)} %bitcast.place, s32[16]{0:T(128)S(1)} %copy-done.1, bf16[128,64,128]{2,1,0:T(8,128)(2,1)S(1)} %copy-done, bf16[528,128]{1,0:T(8,128)(2,1)S(1)} %collective-permute-done.4.refs_0_, ...), custom_call_target="tpu_custom_call" | custom-call | flops 671088640 | bytes 1703936 | tf_op jit(solution)/shard_map/attend/pallas_call | solution.py:194
  35.8 1.3 %collective-permute-done.11.refs_2_ = bf16[768,128]{1,0:T(8,128)(2,1)S(1)} collective-permute-done((bf16[768,128]{1,0:T(8,128)(2,1)S(1)}, bf16[768,128]{1,0:T(8,128)(2,1)S(1)}, u32[]{:S(2)}, u32[]{:S(2)}) %collective-permute-start.11) | collective-permute-done | bytes 196640 | tf_op jit(solution)/shard_map/ppermute | solution.py:219
  37.1 3.7 %attend.4.refs_7_ = bf16[3,128,8,128]{3,2,1,0:T(8,128)(2,1)S(1)} custom-call(s32[1]{0:T(128)} %bitcast.place, s32[16]{0:T(128)S(1)} %copy-done.1, bf16[128,64,128]{2,1,0:T(8,128)(2,1)S(1)} %copy-done, bf16[768,128]{1,0:T(8,128)(2,1)S(1)} %collective-permute-done.8.refs_0_, bf16[768,128]{1,0:T(8,128)(2,1)S(1)} %collective-permute-done.9.refs_1_, ...), custom_call_target="tpu_custom_call" | custom-call | flops 1006632960 | bytes 2555904 | tf_op jit(solution)/shard_map/attend/pallas_call | solution.py:194
  40.8 0.0 collective-permute-done.3.refs_2_
  40.8 4.5 %attend.5 = bf16[128,64,128]{2,1,0:T(8,128)(2,1)} custom-call(s32[1]{0:T(128)} %bitcast.place, s32[16]{0:T(128)S(1)} %copy-done.1, bf16[128,64,128]{2,1,0:T(8,128)(2,1)S(1)} %copy-done, bf16[768,128]{1,0:T(8,128)(2,1)S(1)} %collective-permute-done.refs_0_, bf16[768,128]{1,0:T(8,128)(2,1)S(1)} %collective-permute-done.1.refs_1_, ...), custom_call_target="tpu_custom_call" | custom-call | flops 1006632960 | bytes 2555904 | tf_op jit(solution)/shard_map/attend/pallas_call | solution.py:194
  (6 shorter events, 0.1 us)
Async XLA Ops:
  0.0 33.0 %copy-start = (bf16[128,64,128]{2,1,0:T(8,128)(2,1)S(1)}, bf16[128,64,128]{2,1,0:T(8,128)(2,1)}, u32[]{:S(2)}) copy-start(bf16[128,64,128]{2,1,0:T(8,128)(2,1)} %q_ref.5) | copy-start | bytes 6291460
  0.0 33.0 %copy-start.1 = (s32[16]{0:T(128)S(1)}, s32[16]{0:T(128)}, u32[]{:S(2)}) copy-start(s32[16]{0:T(128)} %counts.5) | copy-start | bytes 196
  1.4 7.7 %collective-permute-start.4 = (bf16[528,128]{1,0:T(8,128)(2,1)S(1)}, bf16[528,128]{1,0:T(8,128)(2,1)S(1)}, u32[]{:S(2)}, u32[]{:S(2)}) collective-permute-start(bf16[528,128]{1,0:T(8,128)(2,1)S(1)} %get-tuple-element.11.refs_4_), channel_id=1, source_target_pairs={{0,4},{1,5},{2,6},{3,7},{4,8},{5,9},{6,10},{7,11},{8,12},{9,13},{1... | collective-permute-start | bytes 405512 | tf_op jit(solution)/shard_map/ppermute | solution.py:224
  3.0 16.8 %collective-permute-start = (bf16[768,128]{1,0:T(8,128)(2,1)S(1)}, bf16[768,128]{1,0:T(8,128)(2,1)S(1)}, u32[]{:S(2)}, u32[]{:S(2)}) collective-permute-start(bf16[768,128]{1,0:T(8,128)(2,1)S(1)} %get-tuple-element.10.refs_4_), channel_id=1, source_target_pairs={{0,4},{1,5},{2,6},{3,7},{4,8},{5,9},{6,10},{7,11},{8,12},{9,13},{1... | collective-permute-start | bytes 589832 | tf_op jit(solution)/shard_map/ppermute | solution.py:224
  4.6 11.9 %collective-permute-start.8 = (bf16[768,128]{1,0:T(8,128)(2,1)S(1)}, bf16[768,128]{1,0:T(8,128)(2,1)S(1)}, u32[]{:S(2)}, u32[]{:S(2)}) collective-permute-start(bf16[768,128]{1,0:T(8,128)(2,1)S(1)} %get-tuple-element.14.refs_4_), channel_id=1, source_target_pairs={{0,4},{1,5},{2,6},{3,7},{4,8},{5,9},{6,10},{7,11},{8,12},{9,13},{1... | collective-permute-start | bytes 589832 | tf_op jit(solution)/shard_map/ppermute | solution.py:224
  9.2 11.1 %collective-permute-start.6 = (bf16[528,128]{1,0:T(8,128)(2,1)S(1)}, bf16[528,128]{1,0:T(8,128)(2,1)S(1)}, u32[]{:S(2)}, u32[]{:S(2)}) collective-permute-start(bf16[528,128]{1,0:T(8,128)(2,1)S(1)} %get-tuple-element.19), channel_id=1, source_target_pairs={{0,1},{1,2},{2,3},{3,0},{4,5},{5,6},{6,7},{7,4},{8,9},{9,10},{10,1... | collective-permute-start | bytes 405512 | tf_op jit(solution)/shard_map/ppermute | solution.py:219
  10.7 12.5 %collective-permute-start.5 = (bf16[528,128]{1,0:T(8,128)(2,1)S(1)}, bf16[528,128]{1,0:T(8,128)(2,1)S(1)}, u32[]{:S(2)}, u32[]{:S(2)}) collective-permute-start(bf16[528,128]{1,0:T(8,128)(2,1)S(1)} %get-tuple-element.20), channel_id=1, source_target_pairs={{0,3},{1,0},{2,1},{3,2},{4,7},{5,4},{6,5},{7,6},{8,11},{9,8},{10,9... | collective-permute-start | bytes 405512 | tf_op jit(solution)/shard_map/ppermute | solution.py:219
  16.5 8.6 %collective-permute-start.10 = (bf16[768,128]{1,0:T(8,128)(2,1)S(1)}, bf16[768,128]{1,0:T(8,128)(2,1)S(1)}, u32[]{:S(2)}, u32[]{:S(2)}) collective-permute-start(bf16[768,128]{1,0:T(8,128)(2,1)S(1)} %get-tuple-element.15), channel_id=1, source_target_pairs={{0,1},{1,2},{2,3},{3,0},{4,5},{5,6},{6,7},{7,4},{8,9},{9,10},{10,1... | collective-permute-start | bytes 589832 | tf_op jit(solution)/shard_map/ppermute | solution.py:219
  18.1 7.8 %collective-permute-start.9 = (bf16[768,128]{1,0:T(8,128)(2,1)S(1)}, bf16[768,128]{1,0:T(8,128)(2,1)S(1)}, u32[]{:S(2)}, u32[]{:S(2)}) collective-permute-start(bf16[768,128]{1,0:T(8,128)(2,1)S(1)} %get-tuple-element.16), channel_id=1, source_target_pairs={{0,3},{1,0},{2,1},{3,2},{4,7},{5,4},{6,5},{7,6},{8,11},{9,8},{10,9... | collective-permute-start | bytes 589832 | tf_op jit(solution)/shard_map/ppermute | solution.py:219
  19.9 8.0 %collective-permute-start.2 = (bf16[768,128]{1,0:T(8,128)(2,1)S(1)}, bf16[768,128]{1,0:T(8,128)(2,1)S(1)}, u32[]{:S(2)}, u32[]{:S(2)}) collective-permute-start(bf16[768,128]{1,0:T(8,128)(2,1)S(1)} %get-tuple-element.17), channel_id=1, source_target_pairs={{0,1},{1,2},{2,3},{3,0},{4,5},{5,6},{6,7},{7,4},{8,9},{9,10},{10,1... | collective-permute-start | bytes 589832 | tf_op jit(solution)/shard_map/ppermute | solution.py:219
  20.2 9.8 %collective-permute-start.1 = (bf16[768,128]{1,0:T(8,128)(2,1)S(1)}, bf16[768,128]{1,0:T(8,128)(2,1)S(1)}, u32[]{:S(2)}, u32[]{:S(2)}) collective-permute-start(bf16[768,128]{1,0:T(8,128)(2,1)S(1)} %get-tuple-element.18), channel_id=1, source_target_pairs={{0,3},{1,0},{2,1},{3,2},{4,7},{5,4},{6,5},{7,6},{8,11},{9,8},{10,9... | collective-permute-start | bytes 589832 | tf_op jit(solution)/shard_map/ppermute | solution.py:219
  23.2 9.8 %collective-permute-start.7 = (bf16[528,128]{1,0:T(8,128)(2,1)S(1)}, bf16[528,128]{1,0:T(8,128)(2,1)S(1)}, u32[]{:S(2)}, u32[]{:S(2)}) collective-permute-start(bf16[528,128]{1,0:T(8,128)(2,1)S(1)} %broadcast_select_fusion.7), channel_id=1, source_target_pairs={{0,1},{1,0},{2,3},{3,2},{4,5},{5,4},{6,7},{7,6},{8,9},{9,8},{10,11... | collective-permute-start | bytes 405512 | tf_op jit(solution)/shard_map/ppermute | solution.py:219
  25.9 11.2 %collective-permute-start.11 = (bf16[768,128]{1,0:T(8,128)(2,1)S(1)}, bf16[768,128]{1,0:T(8,128)(2,1)S(1)}, u32[]{:S(2)}, u32[]{:S(2)}) collective-permute-start(bf16[768,128]{1,0:T(8,128)(2,1)S(1)} %broadcast_select_fusion.2), channel_id=1, source_target_pairs={{0,1},{1,0},{2,3},{3,2},{4,5},{5,4},{6,7},{7,6},{8,9},{9,8},{10,11... | collective-permute-start | bytes 589832 | tf_op jit(solution)/shard_map/ppermute | solution.py:219
  30.1 10.7 %collective-permute-start.3 = (bf16[768,128]{1,0:T(8,128)(2,1)S(1)}, bf16[768,128]{1,0:T(8,128)(2,1)S(1)}, u32[]{:S(2)}, u32[]{:S(2)}) collective-permute-start(bf16[768,128]{1,0:T(8,128)(2,1)S(1)} %broadcast_select_fusion.3), channel_id=1, source_target_pairs={{0,1},{1,0},{2,3},{3,2},{4,5},{5,4},{6,7},{7,6},{8,9},{9,8},{10,11... | collective-permute-start | bytes 589832 | tf_op jit(solution)/shard_map/ppermute | solution.py:219

commit v4 on v3

--- a/solution.py
+++ b/solution.py
@@ -65,6 +65,24 @@
     )
 
 
+def prepare_kernel(payload, select):
+    position = lax.broadcasted_iota(jnp.int32, select.shape, 0) // GROUP
+    column = lax.broadcasted_iota(jnp.int32, select.shape, 1)
+    select[...] = jnp.where(position == column, 1.0, 0.0).astype(jnp.bfloat16)
+
+
+def prepare(payload, shard):
+    vmem = pl.BlockSpec(memory_space=pltpu.VMEM)
+    return pl.pallas_call(
+        prepare_kernel,
+        out_shape=jax.ShapeDtypeStruct((shard * GROUP, shard), jnp.bfloat16),
+        in_specs=[vmem],
+        out_specs=vmem,
+        compiler_params=pltpu.CompilerParams(vmem_limit_bytes=8 << 20),
+        name="prepare",
+    )(payload)
+
+
 def fill_mask(place, counts, docs, mask, shard):
     me = place[0]
     query_doc = jnp.broadcast_to(docs[-1].astype(jnp.float32), (shard, shard))
@@ -79,7 +97,7 @@
         mask[i * shard : (i + 1) * shard, :] = jnp.where(allowed, 0.0, MASKED).astype(jnp.bfloat16)
 
 
-def attend_kernel(place, counts, q_ref, *refs, scale, starts, heads, makes_mask):
+def attend_kernel(place, counts, select, q_ref, *refs, scale, starts, heads, makes_mask):
     blocks = len(BACK)
     parts, refs = refs[:blocks], list(refs[blocks:])
     shard, _, width = q_ref.shape
@@ -93,14 +111,14 @@
         mask = refs.pop(0)
         at = 2 * heads * shard
         fill_mask(place, counts, [p[at : at + 1, :] for p in parts], mask, shard)
-    select, key_window, value_window = refs[:3]
+    key_window, value_window = refs[:2]
     copies = []
 
     def send(source, rows, head):
         at = head * group
         copies.append(
             pltpu.make_async_copy(
-                source, out_ref.at[rows, at : at + group, :], refs[4].at[len(copies)]
+                source, out_ref.at[rows, at : at + group, :], refs[3].at[len(copies)]
             )
         )
         copies[-1].start()
@@ -108,10 +126,7 @@
     for other, start in zip(others, starts):
         for j in range(other.shape[0]):
             send(other.at[j], slice(0, shard), start + j)
-    mixed_heads = refs[3] if last else out_ref
-    position = lax.broadcasted_iota(jnp.int32, (shard * group, shard), 0) // group
-    column = lax.broadcasted_iota(jnp.int32, (shard * group, shard), 1)
-    select[...] = jnp.where(position == column, 1.0, 0.0).astype(jnp.bfloat16)
+    mixed_heads = refs[2] if last else out_ref
     for j in range(heads):
         key_window[j, :, width:] = mask[...]
         for i in range(blocks):
@@ -160,13 +175,13 @@
         copy.wait()
 
 
-def attend(place, counts, queries, parts, starts, heads, mask, others):
+def attend(place, counts, select, queries, parts, starts, heads, mask, others):
     shard, _, width = queries.shape
     window = len(BACK) * shard
     last = starts[-1] + heads == sum(SPLIT)
     vmem = pl.BlockSpec(memory_space=pltpu.VMEM)
-    in_specs = [pl.BlockSpec(memory_space=pltpu.SMEM)] * 2 + [vmem] * (1 + len(BACK))
-    operands = [place, counts, queries, *parts]
+    in_specs = [pl.BlockSpec(memory_space=pltpu.SMEM)] * 2 + [vmem] * (2 + len(BACK))
+    operands = [place, counts, select, queries, *parts]
     mixed = (heads, shard, GROUP, width)
     if last:
         out_shape = [jax.ShapeDtypeStruct(queries.shape, jnp.bfloat16)]
@@ -181,7 +196,6 @@
         operands.append(mask)
         in_specs.append(vmem)
     scratch = [
-        pltpu.VMEM((shard * GROUP, shard), jnp.bfloat16),
         pltpu.VMEM((heads, window, 2 * width), jnp.bfloat16),
         pltpu.VMEM((heads, window, width), jnp.bfloat16),
     ]
@@ -243,11 +257,12 @@
     parts = []
     for own in pack(doc_ids, keys, values):
         parts.append(earlier_shards(own, x, False))
+    select = prepare(parts[0][-1], queries.shape[0])
     mask = None
     starts, mixed = [], []
     for i, (heads, part) in enumerate(zip(SPLIT, parts)):
         starts.append(sum(SPLIT[:i]))
-        out, mask = attend(place, counts, queries, part, starts, heads, mask, mixed)
+        out, mask = attend(place, counts, select, queries, part, starts, heads, mask, mixed)
         mixed.append(out)
     return mixed[-1]
 

time: 45.5 us -> 45.5 us (level)
  the two profiles are of different devices: /device:TPU:64 before, /device:TPU:160 now
where the time goes in v4:
time: 45.5 us; the launch traced here: 45.4 us
  starting transfers between devices  16.3 us (36%)
  waiting for transfers between devices  16.3 us (36%)
  Pallas kernels  12.4 us (27%)
    ppermute x9, starting transfers between devices, row_permute(): lax.ppermute(array, 'seq', [(4 * r + i, 4 * r + j) for r in range(rows) f...  11.8 us
    pallas_call x3, Pallas kernels, attend(): pl.pallas_call(functools.partial(attend_kernel, scale=math.log2(math.e) /...  11.1 us
    ppermute x9, waiting for transfers between devices, row_permute(): lax.ppermute(array, 'seq', [(4 * r + i, 4 * r + j) for r in range(rows) f...  9.06 us
    ppermute x3, waiting for transfers between devices, earlier_shards(): back4 = lax.ppermute(own, 'seq', [(i, (i + 4) % size) for i in range(size)])  7.25 us
    ppermute x3, starting transfers between devices, earlier_shards(): back4 = lax.ppermute(own, 'seq', [(i, (i + 4) % size) for i in range(size)])  4.51 us
    pallas_call x1, Pallas kernels, pack(): pl.pallas_call(pack_kernel, out_shape=[jax.ShapeDtypeStruct((r, width), j...  1.22 us
  transfers between devices with their start and end apart: 12, of which 8 were waited for; matrix products, arithmetic and copies ran while one was open for 0% of the time, Pallas kernels for 15%

profile of v4, /device:TPU:160, one launch (start us, length us, event | category | flops | bytes accessed | tf_op | source)
XLA Modules:
  0.0 45.4 jit_solution(18358696293897754989)
XLA Ops:
  0.0 1.2 %pack.1 = (bf16[528,128]{1,0:T(8,128)(2,1)S(1)}, bf16[768,128]{1,0:T(8,128)(2,1)S(1)}, bf16[768,128]{1,0:T(8,128)(2,1)S(1)}) custom-call(s32[1,128]{1,0:T(1,128)} %bitcast.2, bf16[128,8,128]{2,1,0:T(8,128)(2,1)} %keys_hbm.1, bf16[128,8,128]{2,1,0:T(8,128)(2,1)} %values_hbm.1), custom_call_target="tpu_custom_call" | custom-call | tf_op jit(solution)/shard_map/pack/pallas_call | solution.py:47
  1.2 0.0 copy-start
  1.2 0.0 copy-start.1
  1.3 1.7 %collective-permute-start.4 = (bf16[528,128]{1,0:T(8,128)(2,1)S(1)}, bf16[528,128]{1,0:T(8,128)(2,1)S(1)}, u32[]{:S(2)}, u32[]{:S(2)}) collective-permute-start(bf16[528,128]{1,0:T(8,128)(2,1)S(1)} %get-tuple-element.10.payload.refs_4_), channel_id=1, source_target_pairs={{0,4},{1,5},{2,6},{3,7},{4,8},{5,9},{6,10},{7,11},{8,12},{9,13},{1... | collective-permute-start | bytes 405512 | tf_op jit(solution)/shard_map/ppermute | solution.py:238
  2.9 1.6 %collective-permute-start = (bf16[768,128]{1,0:T(8,128)(2,1)S(1)}, bf16[768,128]{1,0:T(8,128)(2,1)S(1)}, u32[]{:S(2)}, u32[]{:S(2)}) collective-permute-start(bf16[768,128]{1,0:T(8,128)(2,1)S(1)} %get-tuple-element.11.refs_4_), channel_id=1, source_target_pairs={{0,4},{1,5},{2,6},{3,7},{4,8},{5,9},{6,10},{7,11},{8,12},{9,13},{1... | collective-permute-start | bytes 589832 | tf_op jit(solution)/shard_map/ppermute | solution.py:238
  4.5 1.3 %collective-permute-start.8 = (bf16[768,128]{1,0:T(8,128)(2,1)S(1)}, bf16[768,128]{1,0:T(8,128)(2,1)S(1)}, u32[]{:S(2)}, u32[]{:S(2)}) collective-permute-start(bf16[768,128]{1,0:T(8,128)(2,1)S(1)} %get-tuple-element.14.refs_4_), channel_id=1, source_target_pairs={{0,4},{1,5},{2,6},{3,7},{4,8},{5,9},{6,10},{7,11},{8,12},{9,13},{1... | collective-permute-start | bytes 589832 | tf_op jit(solution)/shard_map/ppermute | solution.py:238
  5.8 3.2 %collective-permute-done.4.refs_0_ = bf16[528,128]{1,0:T(8,128)(2,1)S(1)} collective-permute-done((bf16[528,128]{1,0:T(8,128)(2,1)S(1)}, bf16[528,128]{1,0:T(8,128)(2,1)S(1)}, u32[]{:S(2)}, u32[]{:S(2)}) %collective-permute-start.4) | collective-permute-done | bytes 135200 | tf_op jit(solution)/shard_map/ppermute | solution.py:238
  9.0 1.6 %collective-permute-start.6 = (bf16[528,128]{1,0:T(8,128)(2,1)S(1)}, bf16[528,128]{1,0:T(8,128)(2,1)S(1)}, u32[]{:S(2)}, u32[]{:S(2)}) collective-permute-start(bf16[528,128]{1,0:T(8,128)(2,1)S(1)} %get-tuple-element.19), channel_id=1, source_target_pairs={{0,1},{1,2},{2,3},{3,0},{4,5},{5,6},{6,7},{7,4},{8,9},{9,10},{10,1... | collective-permute-start | bytes 405512 | tf_op jit(solution)/shard_map/ppermute | solution.py:233
  10.6 1.7 %collective-permute-start.5 = (bf16[528,128]{1,0:T(8,128)(2,1)S(1)}, bf16[528,128]{1,0:T(8,128)(2,1)S(1)}, u32[]{:S(2)}, u32[]{:S(2)}) collective-permute-start(bf16[528,128]{1,0:T(8,128)(2,1)S(1)} %get-tuple-element.20), channel_id=1, source_target_pairs={{0,3},{1,0},{2,1},{3,2},{4,7},{5,4},{6,5},{7,6},{8,11},{9,8},{10,9... | collective-permute-start | bytes 405512 | tf_op jit(solution)/shard_map/ppermute | solution.py:233
  12.3 4.0 %collective-permute-done.8.refs_0_ = bf16[768,128]{1,0:T(8,128)(2,1)S(1)} collective-permute-done((bf16[768,128]{1,0:T(8,128)(2,1)S(1)}, bf16[768,128]{1,0:T(8,128)(2,1)S(1)}, u32[]{:S(2)}, u32[]{:S(2)}) %collective-permute-start.8) | collective-permute-done | bytes 196640 | tf_op jit(solution)/shard_map/ppermute | solution.py:238
  16.4 1.6 %collective-permute-start.10 = (bf16[768,128]{1,0:T(8,128)(2,1)S(1)}, bf16[768,128]{1,0:T(8,128)(2,1)S(1)}, u32[]{:S(2)}, u32[]{:S(2)}) collective-permute-start(bf16[768,128]{1,0:T(8,128)(2,1)S(1)} %get-tuple-element.15), channel_id=1, source_target_pairs={{0,1},{1,2},{2,3},{3,0},{4,5},{5,6},{6,7},{7,4},{8,9},{9,10},{10,1... | collective-permute-start | bytes 589832 | tf_op jit(solution)/shard_map/ppermute | solution.py:233
  18.0 1.7 %collective-permute-start.9 = (bf16[768,128]{1,0:T(8,128)(2,1)S(1)}, bf16[768,128]{1,0:T(8,128)(2,1)S(1)}, u32[]{:S(2)}, u32[]{:S(2)}) collective-permute-start(bf16[768,128]{1,0:T(8,128)(2,1)S(1)} %get-tuple-element.16), channel_id=1, source_target_pairs={{0,3},{1,0},{2,1},{3,2},{4,7},{5,4},{6,5},{7,6},{8,11},{9,8},{10,9... | collective-permute-start | bytes 589832 | tf_op jit(solution)/shard_map/ppermute | solution.py:233
  19.7 0.0 collective-permute-done.refs_0_
  19.7 0.4 collective-permute-start.2
  20.1 0.0 collective-permute-done.6.refs_3_
  20.1 3.0 %collective-permute-start.1 = (bf16[768,128]{1,0:T(8,128)(2,1)S(1)}, bf16[768,128]{1,0:T(8,128)(2,1)S(1)}, u32[]{:S(2)}, u32[]{:S(2)}) collective-permute-start(bf16[768,128]{1,0:T(8,128)(2,1)S(1)} %get-tuple-element.18), channel_id=1, source_target_pairs={{0,3},{1,0},{2,1},{3,2},{4,7},{5,4},{6,5},{7,6},{8,11},{9,8},{10,9... | collective-permute-start | bytes 589832 | tf_op jit(solution)/shard_map/ppermute | solution.py:233
  23.1 0.0 collective-permute-done.5.refs_1_
  23.1 0.1 collective-permute-start.7
  23.2 1.8 %collective-permute-done.10.refs_3_ = bf16[768,128]{1,0:T(8,128)(2,1)S(1)} collective-permute-done((bf16[768,128]{1,0:T(8,128)(2,1)S(1)}, bf16[768,128]{1,0:T(8,128)(2,1)S(1)}, u32[]{:S(2)}, u32[]{:S(2)}) %collective-permute-start.10) | collective-permute-done | bytes 196640 | tf_op jit(solution)/shard_map/ppermute | solution.py:233
  24.9 0.8 %collective-permute-done.9.refs_1_ = bf16[768,128]{1,0:T(8,128)(2,1)S(1)} collective-permute-done((bf16[768,128]{1,0:T(8,128)(2,1)S(1)}, bf16[768,128]{1,0:T(8,128)(2,1)S(1)}, u32[]{:S(2)}, u32[]{:S(2)}) %collective-permute-start.9) | collective-permute-done | bytes 196640 | tf_op jit(solution)/shard_map/ppermute | solution.py:233
  25.8 1.5 %collective-permute-start.11 = (bf16[768,128]{1,0:T(8,128)(2,1)S(1)}, bf16[768,128]{1,0:T(8,128)(2,1)S(1)}, u32[]{:S(2)}, u32[]{:S(2)}) collective-permute-start(bf16[768,128]{1,0:T(8,128)(2,1)S(1)} %broadcast_select_fusion.2), channel_id=1, source_target_pairs={{0,1},{1,0},{2,3},{3,2},{4,5},{5,4},{6,7},{7,6},{8,9},{9,8},{10,11... | collective-permute-start | bytes 589832 | tf_op jit(solution)/shard_map/ppermute | solution.py:233
  27.2 0.5 %collective-permute-done.2.refs_3_ = bf16[768,128]{1,0:T(8,128)(2,1)S(1)} collective-permute-done((bf16[768,128]{1,0:T(8,128)(2,1)S(1)}, bf16[768,128]{1,0:T(8,128)(2,1)S(1)}, u32[]{:S(2)}, u32[]{:S(2)}) %collective-permute-start.2) | collective-permute-done | bytes 196640 | tf_op jit(solution)/shard_map/ppermute | solution.py:233
  27.7 2.2 %collective-permute-done.1.refs_1_ = bf16[768,128]{1,0:T(8,128)(2,1)S(1)} collective-permute-done((bf16[768,128]{1,0:T(8,128)(2,1)S(1)}, bf16[768,128]{1,0:T(8,128)(2,1)S(1)}, u32[]{:S(2)}, u32[]{:S(2)}) %collective-permute-start.1) | collective-permute-done | bytes 196640 | tf_op jit(solution)/shard_map/ppermute | solution.py:233
  30.0 0.3 collective-permute-start.3
  30.3 0.1 prepare.1.select
  30.3 2.5 %collective-permute-done.7.refs_2_ = bf16[528,128]{1,0:T(8,128)(2,1)S(1)} collective-permute-done((bf16[528,128]{1,0:T(8,128)(2,1)S(1)}, bf16[528,128]{1,0:T(8,128)(2,1)S(1)}, u32[]{:S(2)}, u32[]{:S(2)}) %collective-permute-start.7) | collective-permute-done | bytes 135200 | tf_op jit(solution)/shard_map/ppermute | solution.py:233
  32.8 0.0 copy-done
  32.8 0.0 copy-done.1
  32.8 2.8 %attend.3 = (bf16[2,128,8,128]{3,2,1,0:T(8,128)(2,1)S(1)}, bf16[640,128]{1,0:T(8,128)(2,1)S(1)}) custom-call(s32[1]{0:T(128)} %bitcast.place, s32[16]{0:T(128)S(1)} %copy-done.1, bf16[1024,128]{1,0:T(8,128)(2,1)S(1)} %prepare.1.select, bf16[128,64,128]{2,1,0:T(8,128)(2,1)S(1)} %copy-done, bf16[528,128]{1,0:T(8,128)(2,1)S(1)} %collective-permute-done.4.refs_0_, ...), custom_call_target="tpu_custom_call" | custom-call | flops 671088640 | bytes 1703936 | tf_op jit(solution)/shard_map/attend/pallas_call | solution.py:208
  35.7 1.3 %collective-permute-done.11.refs_2_ = bf16[768,128]{1,0:T(8,128)(2,1)S(1)} collective-permute-done((bf16[768,128]{1,0:T(8,128)(2,1)S(1)}, bf16[768,128]{1,0:T(8,128)(2,1)S(1)}, u32[]{:S(2)}, u32[]{:S(2)}) %collective-permute-start.11) | collective-permute-done | bytes 196640 | tf_op jit(solution)/shard_map/ppermute | solution.py:233
  37.0 3.8 %attend.4.refs_7_ = bf16[3,128,8,128]{3,2,1,0:T(8,128)(2,1)S(1)} custom-call(s32[1]{0:T(128)} %bitcast.place, s32[16]{0:T(128)S(1)} %copy-done.1, bf16[1024,128]{1,0:T(8,128)(2,1)S(1)} %prepare.1.select, bf16[128,64,128]{2,1,0:T(8,128)(2,1)S(1)} %copy-done, bf16[768,128]{1,0:T(8,128)(2,1)S(1)} %collective-permute-done.8.refs_0_, ...), custom_call_target="tpu_custom_call" | custom-call | flops 1006632960 | bytes 2555904 | tf_op jit(solution)/shard_map/attend/pallas_call | solution.py:208
  40.8 0.0 collective-permute-done.3.refs_2_
  40.8 4.5 %attend.5 = bf16[128,64,128]{2,1,0:T(8,128)(2,1)} custom-call(s32[1]{0:T(128)} %bitcast.place, s32[16]{0:T(128)S(1)} %copy-done.1, bf16[1024,128]{1,0:T(8,128)(2,1)S(1)} %prepare.1.select, bf16[128,64,128]{2,1,0:T(8,128)(2,1)S(1)} %copy-done, bf16[768,128]{1,0:T(8,128)(2,1)S(1)} %collective-permute-done.refs_0_, ...), custom_call_target="tpu_custom_call" | custom-call | flops 1006632960 | bytes 2555904 | tf_op jit(solution)/shard_map/attend/pallas_call | solution.py:208
  (6 shorter events, 0.1 us)
Async XLA Ops:
  1.2 31.6 %copy-start = (bf16[128,64,128]{2,1,0:T(8,128)(2,1)S(1)}, bf16[128,64,128]{2,1,0:T(8,128)(2,1)}, u32[]{:S(2)}) copy-start(bf16[128,64,128]{2,1,0:T(8,128)(2,1)} %q_ref.5) | copy-start | bytes 6291460
  1.2 31.6 %copy-start.1 = (s32[16]{0:T(128)S(1)}, s32[16]{0:T(128)}, u32[]{:S(2)}) copy-start(s32[16]{0:T(128)} %counts.5) | copy-start | bytes 196
  1.3 7.7 %collective-permute-start.4 = (bf16[528,128]{1,0:T(8,128)(2,1)S(1)}, bf16[528,128]{1,0:T(8,128)(2,1)S(1)}, u32[]{:S(2)}, u32[]{:S(2)}) collective-permute-start(bf16[528,128]{1,0:T(8,128)(2,1)S(1)} %get-tuple-element.10.payload.refs_4_), channel_id=1, source_target_pairs={{0,4},{1,5},{2,6},{3,7},{4,8},{5,9},{6,10},{7,11},{8,12},{9,13},{1... | collective-permute-start | bytes 405512 | tf_op jit(solution)/shard_map/ppermute | solution.py:238
  2.9 16.8 %collective-permute-start = (bf16[768,128]{1,0:T(8,128)(2,1)S(1)}, bf16[768,128]{1,0:T(8,128)(2,1)S(1)}, u32[]{:S(2)}, u32[]{:S(2)}) collective-permute-start(bf16[768,128]{1,0:T(8,128)(2,1)S(1)} %get-tuple-element.11.refs_4_), channel_id=1, source_target_pairs={{0,4},{1,5},{2,6},{3,7},{4,8},{5,9},{6,10},{7,11},{8,12},{9,13},{1... | collective-permute-start | bytes 589832 | tf_op jit(solution)/shard_map/ppermute | solution.py:238
  4.5 11.9 %collective-permute-start.8 = (bf16[768,128]{1,0:T(8,128)(2,1)S(1)}, bf16[768,128]{1,0:T(8,128)(2,1)S(1)}, u32[]{:S(2)}, u32[]{:S(2)}) collective-permute-start(bf16[768,128]{1,0:T(8,128)(2,1)S(1)} %get-tuple-element.14.refs_4_), channel_id=1, source_target_pairs={{0,4},{1,5},{2,6},{3,7},{4,8},{5,9},{6,10},{7,11},{8,12},{9,13},{1... | collective-permute-start | bytes 589832 | tf_op jit(solution)/shard_map/ppermute | solution.py:238
  9.0 11.1 %collective-permute-start.6 = (bf16[528,128]{1,0:T(8,128)(2,1)S(1)}, bf16[528,128]{1,0:T(8,128)(2,1)S(1)}, u32[]{:S(2)}, u32[]{:S(2)}) collective-permute-start(bf16[528,128]{1,0:T(8,128)(2,1)S(1)} %get-tuple-element.19), channel_id=1, source_target_pairs={{0,1},{1,2},{2,3},{3,0},{4,5},{5,6},{6,7},{7,4},{8,9},{9,10},{10,1... | collective-permute-start | bytes 405512 | tf_op jit(solution)/shard_map/ppermute | solution.py:233
  10.6 12.5 %collective-permute-start.5 = (bf16[528,128]{1,0:T(8,128)(2,1)S(1)}, bf16[528,128]{1,0:T(8,128)(2,1)S(1)}, u32[]{:S(2)}, u32[]{:S(2)}) collective-permute-start(bf16[528,128]{1,0:T(8,128)(2,1)S(1)} %get-tuple-element.20), channel_id=1, source_target_pairs={{0,3},{1,0},{2,1},{3,2},{4,7},{5,4},{6,5},{7,6},{8,11},{9,8},{10,9... | collective-permute-start | bytes 405512 | tf_op jit(solution)/shard_map/ppermute | solution.py:233
  16.4 8.6 %collective-permute-start.10 = (bf16[768,128]{1,0:T(8,128)(2,1)S(1)}, bf16[768,128]{1,0:T(8,128)(2,1)S(1)}, u32[]{:S(2)}, u32[]{:S(2)}) collective-permute-start(bf16[768,128]{1,0:T(8,128)(2,1)S(1)} %get-tuple-element.15), channel_id=1, source_target_pairs={{0,1},{1,2},{2,3},{3,0},{4,5},{5,6},{6,7},{7,4},{8,9},{9,10},{10,1... | collective-permute-start | bytes 589832 | tf_op jit(solution)/shard_map/ppermute | solution.py:233
  18.0 7.8 %collective-permute-start.9 = (bf16[768,128]{1,0:T(8,128)(2,1)S(1)}, bf16[768,128]{1,0:T(8,128)(2,1)S(1)}, u32[]{:S(2)}, u32[]{:S(2)}) collective-permute-start(bf16[768,128]{1,0:T(8,128)(2,1)S(1)} %get-tuple-element.16), channel_id=1, source_target_pairs={{0,3},{1,0},{2,1},{3,2},{4,7},{5,4},{6,5},{7,6},{8,11},{9,8},{10,9... | collective-permute-start | bytes 589832 | tf_op jit(solution)/shard_map/ppermute | solution.py:233
  19.7 8.0 %collective-permute-start.2 = (bf16[768,128]{1,0:T(8,128)(2,1)S(1)}, bf16[768,128]{1,0:T(8,128)(2,1)S(1)}, u32[]{:S(2)}, u32[]{:S(2)}) collective-permute-start(bf16[768,128]{1,0:T(8,128)(2,1)S(1)} %get-tuple-element.17), channel_id=1, source_target_pairs={{0,1},{1,2},{2,3},{3,0},{4,5},{5,6},{6,7},{7,4},{8,9},{9,10},{10,1... | collective-permute-start | bytes 589832 | tf_op jit(solution)/shard_map/ppermute | solution.py:233
  20.1 9.8 %collective-permute-start.1 = (bf16[768,128]{1,0:T(8,128)(2,1)S(1)}, bf16[768,128]{1,0:T(8,128)(2,1)S(1)}, u32[]{:S(2)}, u32[]{:S(2)}) collective-permute-start(bf16[768,128]{1,0:T(8,128)(2,1)S(1)} %get-tuple-element.18), channel_id=1, source_target_pairs={{0,3},{1,0},{2,1},{3,2},{4,7},{5,4},{6,5},{7,6},{8,11},{9,8},{10,9... | collective-permute-start | bytes 589832 | tf_op jit(solution)/shard_map/ppermute | solution.py:233
  23.1 9.8 %collective-permute-start.7 = (bf16[528,128]{1,0:T(8,128)(2,1)S(1)}, bf16[528,128]{1,0:T(8,128)(2,1)S(1)}, u32[]{:S(2)}, u32[]{:S(2)}) collective-permute-start(bf16[528,128]{1,0:T(8,128)(2,1)S(1)} %broadcast_select_fusion.7), channel_id=1, source_target_pairs={{0,1},{1,0},{2,3},{3,2},{4,5},{5,4},{6,7},{7,6},{8,9},{9,8},{10,11... | collective-permute-start | bytes 405512 | tf_op jit(solution)/shard_map/ppermute | solution.py:233
  25.8 11.2 %collective-permute-start.11 = (bf16[768,128]{1,0:T(8,128)(2,1)S(1)}, bf16[768,128]{1,0:T(8,128)(2,1)S(1)}, u32[]{:S(2)}, u32[]{:S(2)}) collective-permute-start(bf16[768,128]{1,0:T(8,128)(2,1)S(1)} %broadcast_select_fusion.2), channel_id=1, source_target_pairs={{0,1},{1,0},{2,3},{3,2},{4,5},{5,4},{6,7},{7,6},{8,9},{9,8},{10,11... | collective-permute-start | bytes 589832 | tf_op jit(solution)/shard_map/ppermute | solution.py:233
  30.0 10.8 %collective-permute-start.3 = (bf16[768,128]{1,0:T(8,128)(2,1)S(1)}, bf16[768,128]{1,0:T(8,128)(2,1)S(1)}, u32[]{:S(2)}, u32[]{:S(2)}) collective-permute-start(bf16[768,128]{1,0:T(8,128)(2,1)S(1)} %broadcast_select_fusion.3), channel_id=1, source_target_pairs={{0,1},{1,0},{2,3},{3,2},{4,5},{5,4},{6,7},{7,6},{8,9},{9,8},{10,11... | collective-permute-start | bytes 589832 | tf_op jit(solution)/shard_map/ppermute | solution.py:233
